TPU v7x, 32 devices: a whole 2x2x4 slice. The times are simulated.
32 devices in a mesh: col: 16 (over z, y, x), lev: 2 (over core).
Axes of the slice: x: 2, y: 2, z: 4, core: 2. Of those that a mesh axis runs over, the one named last changes fastest.
Arguments:
- perturbations: float32 [80, 16, 16384], P(None, 'lev', 'col'), may hold values from -0.625 to 0.625
- gradient: float32 [32, 16, 16384], P(None, 'lev', 'col'), may hold values from -2 to 2
- horizontal: float32 [20, 16384], P(None, 'col'), may hold values from -50 to 50
- area: float32 [16384], P('col'), may hold values from 1 to 60
- vertical: float32 [20, 16], P(None, 'lev'), may hold values from -1.25 to 1.25
Outputs:
- increment: float32 [32, 16, 16384], P(None, 'lev', 'col')
- background: float32 [32], replicated
All inputs are finite; a program needn't handle non-finite values.
Results may differ from a plain program's by a relative error of at most 0.0003.
Values sent between devices are 32-bit elements; how exact they have to be, the bound alone decides.
A program may use at most 128 MiB of HBM per device.

v0:
```python
import functools

import jax
import jax.numpy as jnp
from jax import lax
from jax.experimental import pallas as pl
from jax.experimental.pallas import tpu as pltpu
from jax.sharding import PartitionSpec as P

LANES = 128
NT = (((1,), (1,)), ((), ()))
TN = (((0,), (0,)), ((), ()))
NN = (((1,), (0,)), ((), ()))


def split(x):
    high = x.astype(jnp.bfloat16)
    low = (x - high.astype(jnp.float32)).astype(jnp.bfloat16)
    return high, low


def adjoint_kernel(sizes, pert_ref, grad_ref, hor_ref, area_ref, terms_ref, stat_ref):
    members, levels, vectors, modes, columns = sizes
    group = LANES // vectors
    chunks = modes // group
    used = chunks * members * levels
    if used < terms_ref.shape[0]:
        terms_ref[used:, :] = jnp.zeros((terms_ref.shape[0] - used, LANES), jnp.float32)
    area = area_ref[...]
    power = jnp.sum(area * hor_ref[...] * hor_ref[...], axis=1, keepdims=True)
    spread_power = jnp.broadcast_to(power, (modes, LANES))
    lane = lax.broadcasted_iota(jnp.int32, (modes, LANES), 1)
    row = lax.broadcasted_iota(jnp.int32, (modes, LANES), 0)
    powers = jnp.sum(jnp.where(lane == row, spread_power, 0.0), axis=0, keepdims=True)
    total = jnp.broadcast_to(jnp.sum(area, axis=1, keepdims=True), (1, LANES))
    stat_row = jnp.where(lane[:1] == modes, total, powers)
    stat_ref[...] = jnp.broadcast_to(stat_row, stat_ref.shape)

    def level(l, carry):
        high, low = split(pert_ref[:, l, :])
        both = jnp.concatenate([high, low], axis=0)
        weighted = grad_ref[:, l, :] * area
        for j in range(chunks):
            products = jnp.concatenate(
                [weighted * hor_ref[b : b + 1, :] for b in range(j * group, (j + 1) * group)],
                axis=0,
            )
            x = jnp.concatenate(split(products), axis=0)
            out = lax.dot_general(both, x, NT, preferred_element_type=jnp.float32)
            terms = out[:members, :LANES] + (out[members:, :LANES] + out[:members, LANES:])
            terms_ref[pl.ds(j * members * levels + l, members, stride=levels), :] = terms
        return carry

    for l in range(levels):
        level(l, 0)


def factor_column(stat, modes):
    lane = lax.broadcasted_iota(jnp.int32, (modes, LANES), 1)
    row = lax.broadcasted_iota(jnp.int32, (modes, LANES), 0)
    wide = jnp.broadcast_to(stat, (modes, LANES))
    power = jnp.sum(jnp.where(lane == row, wide, 0.0), axis=1, keepdims=True)
    area = jnp.sum(jnp.where(lane == modes, wide, 0.0), axis=1, keepdims=True)
    return 1.0 / jnp.sqrt(modes * (power / area + 1e-06)), area


def exchange_kernel(
    sizes, n, terms_ref, stat_ref, vert_ref, vert_t_ref, lifted_ref, parts_ref, total_ref,
    first_a, first_b, second, third, stats, reduced, verticals, weights,
    send_h, recv_h, send_g, recv_g, send_s, recv_s, send_l, recv_l, send_b, recv_b,
    send_p, recv_p,
):
    members, levels, vectors, modes, columns = sizes
    group = LANES // vectors
    chunks = modes // group
    vmodes = vert_ref.shape[0]
    rows = terms_ref.shape[3]
    tiles = rows // levels
    outer = n // 4
    rows_a = first_a.shape[2]
    half_a = pl.ds(0, rows_a)
    half_b = pl.ds(rows_a, rows - rows_a)
    me = lax.axis_index("col")
    lev = lax.axis_index("lev")
    other = 1 - lev
    x = lax.rem(me, 2)
    y = lax.rem(lax.div(me, 2), 2)
    h = lax.div(me, 4)
    not_x, not_y = 1 - x, 1 - y
    x_peer = (4 * h + 2 * y + not_x, lev)
    y_peer = (4 * h + 2 * not_y + x, lev)
    mesh_id = pl.DeviceIdType.MESH
    barrier = pltpu.get_barrier_semaphore()

    def greet(p, carry):
        pl.semaphore_signal(
            barrier, inc=1, device_id=(lax.rem(me + p, n), lev), device_id_type=mesh_id
        )
        return carry

    lax.fori_loop(1, n, greet, 0)
    pl.semaphore_signal(barrier, inc=1, device_id=(me, other), device_id_type=mesh_id)
    pl.semaphore_wait(barrier, n)

    def remote(src, dst, send, recv, device):
        return pltpu.make_async_remote_copy(
            src_ref=src, dst_ref=dst, send_sem=send, recv_sem=recv,
            device_id=device, device_id_type=mesh_id,
        )

    def half_copy(i, src, dst, device):
        return remote(src, dst, send_h.at[i], recv_h.at[i], device)

    def outer_copy(p):
        there = lax.rem(h + p, outer)
        device = (4 * there + 2 * y + x, lev)
        return remote(second.at[there], third.at[p], send_g.at[p], recv_g.at[p], device)

    def stat_copy(p, slot):
        peer = lax.rem(me + p, n)
        return remote(stat_ref, stats.at[slot], send_s.at[p], recv_s.at[p], (peer, lev))

    def lifted_copy(p, slot):
        there = lax.rem(h + p, outer)
        device = (4 * there + 2 * y + x, lev)
        block = lifted_ref.at[slot, y, x]
        return remote(block, block, send_l.at[p], recv_l.at[p], device)

    def part_copy(p, slot):
        peer = lax.rem(me + p, n)
        return remote(
            parts_ref.at[slot], parts_ref.at[slot], send_b.at[p], recv_b.at[p], (peer, lev)
        )

    one_a = half_copy(0, terms_ref.at[:, :, not_x, half_a], first_a, x_peer)
    one_b = half_copy(1, terms_ref.at[:, not_y, :, half_b], first_b, y_peer)
    one_a.start()
    one_b.start()

    def start_stats(p, carry):
        stat_copy(p, me).start()
        return carry

    lax.fori_loop(1, n, start_stats, 0)
    vert_copy = remote(
        vert_ref, verticals.at[lev], send_p.at[0], recv_p.at[0], (me, other)
    )
    vert_copy.start()
    stats[me] = stat_ref[...]
    verticals[lev] = vert_ref[...]

    def add_a(i, carry):
        first_a[i, not_y] += terms_ref[i, not_y, x, half_a]
        return carry

    def add_b(i, carry):
        first_b[i, not_x] += terms_ref[i, y, not_x, half_b]
        return carry

    two_a = half_copy(2, first_a.at[:, not_y], second.at[:, half_a], y_peer)
    two_b = half_copy(3, first_b.at[:, not_x], second.at[:, half_b], x_peer)
    one_a.wait_recv()
    lax.fori_loop(0, outer, add_a, 0)
    two_a.start()
    one_b.wait_recv()
    lax.fori_loop(0, outer, add_b, 0)
    two_b.start()

    def take_stats(p, carry):
        stat_copy(p, lax.rem(me + n - p, n)).wait_recv()
        return carry

    lax.fori_loop(1, n, take_stats, 0)
    two_a.wait_recv()
    two_b.wait_recv()

    def add_second(there):
        second[there, half_a] += terms_ref[there, y, x, half_a] + first_a[there, y]
        second[there, half_b] += terms_ref[there, y, x, half_b] + first_b[there, x]

    def send_outer(p, carry):
        add_second(lax.rem(h + p, outer))
        outer_copy(p).start()
        return carry

    lax.fori_loop(1, outer, send_outer, 0)
    add_second(h)
    reduced[lev] = second[h]

    def take(p, carry):
        outer_copy(p).wait_recv()
        reduced[lev] += third[p]
        return carry

    lax.fori_loop(1, outer, take, 0)
    pair_copy = remote(
        reduced.at[lev], reduced.at[lev], send_p.at[1], recv_p.at[1], (me, other)
    )
    pair_copy.start()

    def add_stat(i, carry):
        return carry + stats[i]

    stat = lax.fori_loop(0, n, add_stat, jnp.zeros(stat_ref.shape, jnp.float32))
    total_ref[...] = stat
    factor, area = factor_column(stat[:1], modes)
    factor = factor / area
    lane = lax.broadcasted_iota(jnp.int32, (modes, LANES), 1)
    row = lax.broadcasted_iota(jnp.int32, (modes, LANES), 0)
    placed = jnp.where(
        lax.div(lane, vectors) == lax.rem(row, group), jnp.broadcast_to(factor, lane.shape), 0.0
    )
    for j in range(chunks):
        weights[j : j + 1, :] = jnp.sum(
            placed[j * group : (j + 1) * group], axis=0, keepdims=True
        )
    remote(
        vert_ref, verticals.at[other], send_p.at[0], recv_p.at[0], (me, other)
    ).wait_recv()
    remote(
        reduced.at[lev], reduced.at[other], send_p.at[1], recv_p.at[1], (me, other)
    ).wait_recv()

    def wide(index):
        block = reduced[index]
        return jnp.concatenate(
            [block[i * levels : (i + 1) * levels] for i in range(tiles)], axis=1
        )

    def dot(a, b):
        return lax.dot_general(
            a, b, NN, precision=lax.Precision.HIGHEST, preferred_element_type=jnp.float32
        )

    control = dot(verticals[0][:, :levels], wide(0)) + dot(verticals[1][:, :levels], wide(1))
    lifted = lax.dot_general(
        vert_t_ref[...], control, TN, precision=lax.Precision.HIGHEST,
        preferred_element_type=jnp.float32,
    )
    part = jnp.zeros((1, LANES), jnp.float32)
    for i in range(tiles):
        lifted_ref[h, y, x, i * levels : (i + 1) * levels, :] = lifted[:, i * LANES : (i + 1) * LANES]
        chunk = jnp.minimum(lax.div(me * tiles + i, members), chunks - 1)
        scaled = control[:, i * LANES : (i + 1) * LANES] * weights[pl.ds(chunk, 1), :]
        part = part + jnp.sum(scaled * scaled, axis=0, keepdims=True)
    parts_ref[me] = jnp.broadcast_to(part, parts_ref.shape[1:])

    def start_lifted(p, carry):
        lifted_copy(p, h).start()
        return carry

    def start_parts(p, carry):
        part_copy(p, me).start()
        return carry

    def take_lifted(p, carry):
        lifted_copy(p, lax.rem(h + outer - p, outer)).wait_recv()
        return carry

    lax.fori_loop(1, outer, start_lifted, 0)
    lax.fori_loop(1, n, start_parts, 0)
    lax.fori_loop(1, outer, take_lifted, 0)

    def gather_copy(i, block, device):
        return half_copy(i, block, block, device)

    three_a = gather_copy(4, lifted_ref.at[:, y, x, half_a], y_peer)
    three_b = gather_copy(5, lifted_ref.at[:, y, x, half_b], x_peer)
    three_a.start()
    three_b.start()
    four_a = gather_copy(6, lifted_ref.at[:, :, x, half_a], x_peer)
    four_b = gather_copy(7, lifted_ref.at[:, y, :, half_b], y_peer)
    gather_copy(4, lifted_ref.at[:, not_y, x, half_a], y_peer).wait_recv()
    four_a.start()
    gather_copy(5, lifted_ref.at[:, y, not_x, half_b], x_peer).wait_recv()
    four_b.start()
    for copy in (one_a, one_b, two_a, two_b, three_a, three_b, vert_copy, pair_copy):
        copy.wait_send()

    def finish(p, carry):
        stat_copy(p, me).wait_send()
        part_copy(p, lax.rem(me + n - p, n)).wait_recv()
        part_copy(p, me).wait_send()
        return carry

    def finish_outer(p, carry):
        outer_copy(p).wait_send()
        lifted_copy(p, h).wait_send()
        return carry

    lax.fori_loop(1, n, finish, 0)
    lax.fori_loop(1, outer, finish_outer, 0)
    gather_copy(6, lifted_ref.at[:, :, not_x, half_a], x_peer).wait_recv()
    gather_copy(7, lifted_ref.at[:, not_y, :, half_b], y_peer).wait_recv()
    four_a.wait_send()
    four_b.wait_send()


def forward_kernel(
    sizes, n, lifted_ref, parts_ref, total_ref, pert_ref, hor_ref, out_ref, bg_ref, scaled_ref
):
    members, levels, vectors, modes, columns = sizes
    group = LANES // vectors
    chunks = modes // group
    width = 256
    part = lax.fori_loop(
        0, n, lambda i, c: c + parts_ref[i], jnp.zeros(parts_ref.shape[1:], jnp.float32)
    )
    folded = part
    for g in range(1, group):
        folded = folded + pltpu.roll(part, g * vectors, 1)
    bg_ref[...] = 0.5 * folded
    factor, area = factor_column(total_ref[:1, :], modes)
    scaled_ref[...] = hor_ref[...] * (factor * (factor / area))

    def level(l, carry):
        lhs = []
        for j in range(chunks):
            high, low = split(
                lifted_ref[pl.ds(j * members * levels + l, members, stride=levels), :]
            )
            lhs.append(jnp.concatenate([high, low, high], axis=0))
        for c in range(0, columns, width):
            high, low = split(pert_ref[:, l, c : c + width])
            rhs = jnp.concatenate([high, high, low], axis=0)
            acc = None
            for j in range(chunks):
                spread = lax.dot_general(lhs[j], rhs, TN, preferred_element_type=jnp.float32)
                for g in range(group):
                    b = j * group + g
                    term = (
                        spread[g * vectors : (g + 1) * vectors]
                        * scaled_ref[b : b + 1, c : c + width]
                    )
                    acc = term if acc is None else acc + term
            out_ref[:, l, c : c + width] = acc
        return carry

    for l in range(levels):
        level(l, 0)


def per_device(perturbations, gradient, horizontal, area, vertical):
    members, levels, columns = perturbations.shape
    vectors = gradient.shape[0]
    modes = horizontal.shape[0]
    vmodes = vertical.shape[0]
    n = lax.axis_size("col")
    sizes = (members, levels, vectors, modes, columns)
    chunks = modes * vectors // LANES
    tiles = -(-chunks * members // n)
    rows = tiles * levels
    outer = n // 4
    rows_a = (tiles + 1) // 2 * levels
    f32 = jnp.float32
    vmem = pl.BlockSpec(memory_space=pltpu.VMEM)

    terms, stat = pl.pallas_call(
        functools.partial(adjoint_kernel, sizes),
        out_shape=(
            jax.ShapeDtypeStruct((n * rows, LANES), f32),
            jax.ShapeDtypeStruct((8, LANES), f32),
        ),
        in_specs=[vmem] * 4,
        out_specs=(vmem, vmem),
        name="adjoint",
    )(perturbations, gradient, horizontal, area.reshape(1, columns))

    vert = vertical * (columns * n)
    vert = jnp.pad(vert, ((0, 0), (0, LANES - levels)))
    dma = pltpu.SemaphoreType.DMA
    lifted, parts, total = pl.pallas_call(
        functools.partial(exchange_kernel, sizes, n),
        out_shape=(
            jax.ShapeDtypeStruct((outer, 2, 2, rows, LANES), f32),
            jax.ShapeDtypeStruct((n, 8, LANES), f32),
            jax.ShapeDtypeStruct((8, LANES), f32),
        ),
        in_specs=[vmem] * 4,
        out_specs=(vmem, vmem, vmem),
        scratch_shapes=[
            pltpu.VMEM((outer, 2, rows_a, LANES), f32),
            pltpu.VMEM((outer, 2, rows - rows_a, LANES), f32),
            pltpu.VMEM((outer, rows, LANES), f32),
            pltpu.VMEM((outer, rows, LANES), f32),
            pltpu.VMEM((n, 8, LANES), f32),
            pltpu.VMEM((2, rows, LANES), f32),
            pltpu.VMEM((2, vmodes, LANES), f32),
            pltpu.VMEM((8, LANES), f32),
            dma((8,)), dma((8,)), dma((outer,)), dma((outer,)), dma((n,)), dma((n,)),
            dma((outer,)), dma((outer,)), dma((n,)), dma((n,)),
            dma((2,)), dma((2,)),
        ],
        compiler_params=pltpu.CompilerParams(collective_id=0, has_side_effects=True),
        name="exchange",
    )(terms.reshape(outer, 2, 2, rows, LANES), stat, vert, vertical)

    increment, background = pl.pallas_call(
        functools.partial(forward_kernel, sizes, n),
        out_shape=(
            jax.ShapeDtypeStruct((vectors, levels, columns), f32),
            jax.ShapeDtypeStruct((8, LANES), f32),
        ),
        in_specs=[vmem] * 5,
        out_specs=(vmem, vmem),
        scratch_shapes=[pltpu.VMEM((modes, columns), f32)],
        name="forward",
    )(lifted.reshape(n * rows, LANES), parts, total, perturbations, horizontal)
    return increment, background[0, :vectors]


def solution(mesh):
    return jax.shard_map(
        per_device,
        mesh=mesh,
        in_specs=(
            P(None, "lev", "col"),
            P(None, "lev", "col"),
            P(None, "col"),
            P("col"),
            P(None, "lev"),
        ),
        out_specs=(P(None, "lev", "col"), P()),
        check_vma=False,
    )
```

profile of v0, /device:TPU:0, one launch (start us, length us, event | category | flops | bytes accessed | tf_op | source)
XLA Modules:
  0.0 100.9 jit_solution(6055029143644696025)
XLA Ops:
  0.6 0.8 copy.9.vert_t_ref
  1.4 0.0 copy-start
  1.4 0.6 pad.4.vert_ref
  2.0 18.9 %adjoint.1 = (f32[3200,128]{1,0:T(8,128)}, f32[8,128]{1,0:T(8,128)}) custom-call(f32[80,8,1024]{2,1,0:T(8,128)} %pert_ref.3, f32[32,8,1024]{2,1,0:T(8,128)} %grad_ref.1, f32[20,1024]{1,0:T(8,128)} %hor_ref.3, f32[1,1024]{1,0:T(1,128)} %bitcast.7), custom_call_target="tpu_custom_call" | custom-call | tf_op jit(solution)/shard_map/adjoint/pallas_call | solution.py:358
  21.0 0.0 copy-done
  21.0 64.0 %exchange.1 = (f32[4,2,2,200,128]{4,3,2,1,0:T(8,128)}, f32[16,8,128]{2,1,0:T(8,128)}, f32[8,128]{1,0:T(8,128)}) custom-call(f32[4,2,2,200,128]{4,3,2,1,0:T(8,128)} %bitcast.6, f32[8,128]{1,0:T(8,128)} %get-tuple-element.10.stat_ref, f32[20,128]{1,0:T(8,128)} %pad.4.vert_ref, f32[20,8]{1,0:T(8,128)} %copy-done), custom_call_target="tpu_custom_call" | custom-call | tf_op jit(solution)/shard_map/exchange/pallas_call | solution.py:372
  85.0 14.7 %forward.1 = (f32[32,8,1024]{2,1,0:T(8,128)}, f32[8,128]{1,0:T(8,128)}) custom-call(f32[3200,128]{1,0:T(8,128)} %bitcast.5, f32[16,8,128]{2,1,0:T(8,128)} %get-tuple-element.12.parts_ref, f32[8,128]{1,0:T(8,128)} %get-tuple-element.13.total_ref, f32[80,8,1024]{2,1,0:T(8,128)} %pert_ref.3, f32[20,1024]{1,0:T(8,128)} %hor_ref.3), custom_call_target="tpu_custom_call" | custom-call | tf_op jit(solution)/shard_map/forward/pallas_call | solution.py:398
  99.7 1.2 %slice_bitcast_fusion = f32[32]{0:T(128)} fusion(f32[8,128]{1,0:T(8,128)} %get-tuple-element.15), kind=kLoop, calls=%fused_computation.1 | loop fusion | bytes 256 | tf_op jit(solution)/shard_map/squeeze | solution.py:409
  (1 shorter events, 0.0 us)
Async XLA Ops:
  1.4 19.6 %copy-start = (f32[20,8]{1,0:T(8,128)}, f32[20,8]{1,0:T(8,128)S(1)}, u32[]{:S(2)}) copy-start(f32[20,8]{1,0:T(8,128)S(1)} %copy.9.vert_t_ref) | copy-start | bytes 1924
where the time goes:
time: 101 us
  Pallas kernels  97.6 us (97%)
  local copies, waits for them, and re-layouts  2.57 us (3%)
    pallas_call x1, Pallas kernels, per_device(): pl.pallas_call(functools.partial(exchange_kernel, sizes, n), out_shape=(j...  64 us
    pallas_call x1, Pallas kernels, per_device(): pl.pallas_call(functools.partial(adjoint_kernel, sizes), out_shape=(jax.S...  18.9 us
    pallas_call x1, Pallas kernels, per_device(): pl.pallas_call(functools.partial(forward_kernel, sizes, n), out_shape=(ja...  14.7 us

commit v1 on v0

v1 whole, which is shorter than its diff:
```python
import functools

import jax
import jax.numpy as jnp
from jax import lax
from jax.experimental import pallas as pl
from jax.experimental.pallas import tpu as pltpu
from jax.sharding import PartitionSpec as P

LANES = 128
NT = (((1,), (1,)), ((), ()))
TN = (((0,), (0,)), ((), ()))
NN = (((1,), (0,)), ((), ()))
UNROLL = 2


def split(x):
    high = x.astype(jnp.bfloat16)
    low = (x - high.astype(jnp.float32)).astype(jnp.bfloat16)
    return high, low


def exact_dot(a, b, dims):
    return lax.dot_general(
        a, b, dims, precision=lax.Precision.HIGHEST, preferred_element_type=jnp.float32
    )


def kernel(
    sizes, n, pert_ref, grad_ref, hor_ref, area_ref, vert_ref, out_ref, bg_ref,
    halves, weighted, acc, terms, first_a, first_b, second, third, reduced, lifted,
    stat_ref, stats, verticals, sums, parts, weights, scaled,
    send_h, recv_h, send_g, recv_g, send_l, recv_l, send_p, recv_p,
    send_s, recv_s, send_b, recv_b, send_v, recv_v,
):
    members, levels, vectors, modes, columns = sizes
    group = LANES // vectors
    chunks = modes // group
    vmodes = vert_ref.shape[1]
    rows = terms.shape[4]
    tiles = rows // levels
    outer = n // 4
    used = members * levels
    me = lax.axis_index("col")
    lev = lax.axis_index("lev")
    other = 1 - lev
    x = lax.rem(me, 2)
    y = lax.rem(lax.div(me, 2), 2)
    h = lax.div(me, 4)
    not_x, not_y = 1 - x, 1 - y
    x_peer = (4 * h + 2 * y + not_x, lev)
    y_peer = (4 * h + 2 * not_y + x, lev)
    mesh_id = pl.DeviceIdType.MESH
    barrier = pltpu.get_barrier_semaphore()

    def greet(p, carry):
        pl.semaphore_signal(
            barrier, inc=1, device_id=(lax.rem(me + p, n), lev), device_id_type=mesh_id
        )
        return carry

    lax.fori_loop(1, n, greet, 0)
    pl.semaphore_signal(barrier, inc=1, device_id=(me, other), device_id_type=mesh_id)

    def remote(src, dst, send, recv, device):
        return pltpu.make_async_remote_copy(
            src_ref=src, dst_ref=dst, send_sem=send, recv_sem=recv,
            device_id=device, device_id_type=mesh_id,
        )

    def halfway(j):
        count = (tiles + 1 - j % 2) // 2 * levels
        return pl.ds(0, count), pl.ds(count, rows - count), count, rows - count

    def half_copy(j, i, src, dst, device):
        return remote(src, dst, send_h.at[j, i], recv_h.at[j, i], device)

    def one(j):
        a, b, na, nb = halfway(j)
        return (
            half_copy(j, 0, terms.at[j, :, :, not_x, a], first_a.at[j, :, :, pl.ds(0, na)], x_peer),
            half_copy(j, 1, terms.at[j, :, not_y, :, b], first_b.at[j, :, :, pl.ds(0, nb)], y_peer),
        )

    def two(j):
        a, b, na, nb = halfway(j)
        return (
            half_copy(j, 2, first_a.at[j, :, not_y, pl.ds(0, na)], second.at[j, :, a], y_peer),
            half_copy(j, 3, first_b.at[j, :, not_x, pl.ds(0, nb)], second.at[j, :, b], x_peer),
        )

    def outer_copy(j, p):
        there = lax.rem(h + p, outer)
        device = (4 * there + 2 * y + x, lev)
        return remote(
            second.at[j, there], third.at[j, p], send_g.at[j, p], recv_g.at[j, p], device
        )

    def pair_copy(j, slot):
        block = reduced.at[j, slot]
        return remote(block, block, send_p.at[j], recv_p.at[j], (me, other))

    def lifted_copy(j, p, slot):
        there = lax.rem(h + p, outer)
        device = (4 * there + 2 * y + x, lev)
        block = lifted.at[j, slot, y, x]
        return remote(block, block, send_l.at[j, p], recv_l.at[j, p], device)

    def three(j, yy, xx):
        a, b, _, _ = halfway(j)
        block_a = lifted.at[j, :, yy, x, a]
        block_b = lifted.at[j, :, y, xx, b]
        return (
            half_copy(j, 4, block_a, block_a, y_peer),
            half_copy(j, 5, block_b, block_b, x_peer),
        )

    def four(j, yy, xx):
        a, b, _, _ = halfway(j)
        block_a = lifted.at[j, :, :, xx, a]
        block_b = lifted.at[j, :, yy, :, b]
        return (
            half_copy(j, 6, block_a, block_a, x_peer),
            half_copy(j, 7, block_b, block_b, y_peer),
        )

    def stat_copy(p, slot):
        peer = lax.rem(me + p, n)
        return remote(stat_ref, stats.at[slot], send_s.at[p], recv_s.at[p], (peer, lev))

    def part_copy(p, slot):
        peer = lax.rem(me + p, n)
        block = parts.at[slot]
        return remote(block, block, send_b.at[p], recv_b.at[p], (peer, lev))

    def vert_copy(slot):
        block = verticals.at[slot]
        return remote(block, block, send_v.at[0], recv_v.at[0], (me, other))

    area = area_ref[...]
    power = jnp.sum(area * hor_ref[...] * hor_ref[...], axis=1, keepdims=True)
    lane = lax.broadcasted_iota(jnp.int32, (modes, LANES), 1)
    row = lax.broadcasted_iota(jnp.int32, (modes, LANES), 0)
    powers = jnp.sum(
        jnp.where(lane == row, jnp.broadcast_to(power, (modes, LANES)), 0.0),
        axis=0, keepdims=True,
    )
    total = jnp.broadcast_to(jnp.sum(area, axis=1, keepdims=True), (1, LANES))
    stat_row = jnp.where(lane[:1] == modes, total, powers)
    stat_ref[...] = jnp.broadcast_to(stat_row, stat_ref.shape)
    verticals[lev] = jnp.zeros(verticals.shape[1:], jnp.float32)
    verticals[lev, :, :vmodes] = vert_ref[...]
    if used < n * rows:
        for j in range(chunks):
            flat = terms.at[j].reshape(n * rows, LANES)
            flat[used:, :] = jnp.zeros((n * rows - used, LANES), jnp.float32)
    for l in range(levels):
        high, low = split(pert_ref[:, l, :])
        halves[l, :members] = high
        halves[l, members:] = low
        weighted[l] = grad_ref[:, l, :] * area

    def over_levels(step):
        def body(i, carry):
            for u in range(UNROLL):
                step(i * UNROLL + u)
            return carry

        lax.fori_loop(0, levels // UNROLL, body, 0)

    def adjoint(j):
        flat = terms.at[j].reshape(n * rows, LANES)

        def step(l):
            base = weighted[l]
            products = jnp.concatenate(
                [base * hor_ref[b : b + 1, :] for b in range(j * group, (j + 1) * group)],
                axis=0,
            )
            both = jnp.concatenate(split(products), axis=0)
            out = lax.dot_general(halves[l], both, NT, preferred_element_type=jnp.float32)
            flat[pl.ds(l, members, stride=levels), :] = out[:members, :LANES] + (
                out[members:, :LANES] + out[:members, LANES:]
            )

        over_levels(step)

    def start(copies):
        for copy in copies:
            copy.start()

    def send_one(j):
        start(one(j))

    def send_two(j):
        a, b, na, nb = halfway(j)
        one_a, one_b = one(j)
        two_a, two_b = two(j)
        one_a.wait_recv()

        def add_a(i, carry):
            first_a[j, i, not_y, :na] += terms[j, i, not_y, x, a]
            return carry

        lax.fori_loop(0, outer, add_a, 0)
        two_a.start()
        one_b.wait_recv()

        def add_b(i, carry):
            first_b[j, i, not_x, :nb] += terms[j, i, y, not_x, b]
            return carry

        lax.fori_loop(0, outer, add_b, 0)
        two_b.start()

    def add_second(j, there):
        a, b, na, nb = halfway(j)
        second[j, there, a] += terms[j, there, y, x, a] + first_a[j, there, y, :na]
        second[j, there, b] += terms[j, there, y, x, b] + first_b[j, there, x, :nb]

    def send_three(j):
        for copy in two(j):
            copy.wait_recv()

        def send_outer(p, carry):
            add_second(j, lax.rem(h + p, outer))
            outer_copy(j, p).start()
            return carry

        lax.fori_loop(1, outer, send_outer, 0)
        add_second(j, h)
        reduced[j, lev] = second[j, h]

    def send_pair(j):
        def take(p, carry):
            outer_copy(j, p).wait_recv()
            reduced[j, lev] += third[j, p]
            return carry

        lax.fori_loop(1, outer, take, 0)
        pair_copy(j, lev).start()

    def mix(j):
        pair_copy(j, other).wait_recv()

        def wide(index):
            block = reduced[j, index]
            return jnp.concatenate(
                [block[i * levels : (i + 1) * levels] for i in range(tiles)], axis=1
            )

        control = exact_dot(verticals[0][:, :vmodes], wide(0), TN) + exact_dot(
            verticals[1][:, :vmodes], wide(1), TN
        )
        raised = exact_dot(vert_ref[...], control, NN)
        square = jnp.zeros((1, LANES), jnp.float32)
        for i in range(tiles):
            lanes = slice(i * LANES, (i + 1) * LANES)
            lifted[j, h, y, x, i * levels : (i + 1) * levels, :] = raised[:, lanes]
            square = square + jnp.sum(
                control[:, lanes] * control[:, lanes], axis=0, keepdims=True
            )
        sums[j : j + 1, :] = square

        def start_lifted(p, carry):
            lifted_copy(j, p, h).start()
            return carry

        lax.fori_loop(1, outer, start_lifted, 0)

    def send_g2(j):
        def take_lifted(p, carry):
            lifted_copy(j, p, lax.rem(h + outer - p, outer)).wait_recv()
            return carry

        lax.fori_loop(1, outer, take_lifted, 0)
        start(three(j, y, x))

    def send_g3(j):
        three_a, three_b = three(j, not_y, not_x)
        four_a, four_b = four(j, y, x)
        three_a.wait_recv()
        four_a.start()
        three_b.wait_recv()
        four_b.start()

    def forward(j):
        for copy in four(j, not_y, not_x):
            copy.wait_recv()
        flat = lifted.at[j].reshape(n * rows, LANES)
        width = 256

        def step(l):
            high, low = split(flat[pl.ds(l, members, stride=levels), :])
            lhs = jnp.concatenate([high, high, low], axis=0)
            for c in range(0, columns, width):
                cols = slice(c, c + width)
                rhs = jnp.concatenate([halves[l, :, cols], halves[l, :members, cols]], axis=0)
                spread = lax.dot_general(lhs, rhs, TN, preferred_element_type=jnp.float32)
                value = None if j == 0 else acc[l, :, cols]
                for g in range(group):
                    b = j * group + g
                    term = spread[g * vectors : (g + 1) * vectors] * scaled[b : b + 1, cols]
                    value = term if value is None else value + term
                if j == chunks - 1:
                    out_ref[:, l, cols] = value
                else:
                    acc[l, :, cols] = value

        if j == chunks - 1:
            for l in range(levels):
                step(l)
        else:
            over_levels(step)

    def take_stats():
        stats[me] = stat_ref[...]

        def take(p, carry):
            stat_copy(p, lax.rem(me + n - p, n)).wait_recv()
            return carry

        lax.fori_loop(1, n, take, 0)
        stat = lax.fori_loop(
            0, n, lambda i, c: c + stats[i], jnp.zeros(stat_ref.shape, jnp.float32)
        )
        spread = jnp.broadcast_to(stat[:1], (modes, LANES))
        power = jnp.sum(jnp.where(lane == row, spread, 0.0), axis=1, keepdims=True)
        whole = jnp.sum(jnp.where(lane == modes, spread, 0.0), axis=1, keepdims=True)
        factor = 1.0 / jnp.sqrt(modes * (power / whole + 1e-06))
        scale = factor * (columns * n / whole)
        scaled[...] = hor_ref[...] * (factor * scale)
        placed = jnp.where(
            lax.div(lane, vectors) == lax.rem(row, group),
            jnp.broadcast_to(scale, lane.shape), 0.0,
        )
        for j in range(chunks):
            weights[j : j + 1, :] = jnp.sum(
                placed[j * group : (j + 1) * group], axis=0, keepdims=True
            )

    def send_parts():
        part = jnp.zeros((1, LANES), jnp.float32)
        for j in range(chunks):
            weight = weights[j : j + 1, :]
            part = part + sums[j : j + 1, :] * weight * weight
        parts[me] = jnp.broadcast_to(part, parts.shape[1:])

        def start_parts(p, carry):
            part_copy(p, me).start()
            return carry

        lax.fori_loop(1, n, start_parts, 0)

    def take_parts():
        def take(p, carry):
            part_copy(p, lax.rem(me + n - p, n)).wait_recv()
            return carry

        lax.fori_loop(1, n, take, 0)
        part = lax.fori_loop(
            0, n, lambda i, c: c + parts[i], jnp.zeros(parts.shape[1:], jnp.float32)
        )
        folded = part
        for g in range(1, group):
            folded = folded + pltpu.roll(part, g * vectors, 1)
        bg_ref[...] = 0.5 * folded

    stages = (adjoint, send_one, send_two, send_three, send_pair, mix, send_g2, send_g3, forward)
    lag = (0, 0, 1, 2, 3, 4, 5, 6, 7)
    for t in range(chunks + lag[-1]):
        if t == 4:
            take_stats()
        j = t - lag[-1]
        if t < chunks:
            adjoint(t)
        if t == 0:
            pl.semaphore_wait(barrier, n)

            def start_stats(p, carry):
                stat_copy(p, me).start()
                return carry

            lax.fori_loop(1, n, start_stats, 0)
            vert_copy(lev).start()
        if t == 3:
            vert_copy(other).wait_recv()
        for stage, late in reversed(tuple(zip(stages[1:-1], lag[1:-1]))):
            if 0 <= t - late < chunks:
                stage(t - late)
        if t - lag[5] == chunks - 1:
            send_parts()
        if 0 <= j < chunks:
            forward(j)
    take_parts()

    for j in range(chunks):
        for copy in one(j) + two(j) + three(j, y, x) + four(j, y, x) + (pair_copy(j, lev),):
            copy.wait_send()

        def finish_outer(p, carry):
            outer_copy(j, p).wait_send()
            lifted_copy(j, p, h).wait_send()
            return carry

        lax.fori_loop(1, outer, finish_outer, 0)

    def finish(p, carry):
        stat_copy(p, me).wait_send()
        part_copy(p, me).wait_send()
        return carry

    lax.fori_loop(1, n, finish, 0)
    vert_copy(lev).wait_send()


def per_device(perturbations, gradient, horizontal, area, vertical):
    members, levels, columns = perturbations.shape
    vectors = gradient.shape[0]
    modes = horizontal.shape[0]
    n = lax.axis_size("col")
    sizes = (members, levels, vectors, modes, columns)
    chunks = modes * vectors // LANES
    tiles = max(2, -(-members // n))
    rows = tiles * levels
    outer = n // 4
    most = (tiles + 1) // 2 * levels
    f32 = jnp.float32
    vmem = pl.BlockSpec(memory_space=pltpu.VMEM)
    dma = pltpu.SemaphoreType.DMA

    increment, background = pl.pallas_call(
        functools.partial(kernel, sizes, n),
        out_shape=(
            jax.ShapeDtypeStruct((vectors, levels, columns), f32),
            jax.ShapeDtypeStruct((8, LANES), f32),
        ),
        in_specs=[vmem] * 5,
        out_specs=(vmem, vmem),
        scratch_shapes=[
            pltpu.VMEM((levels, 2 * members, columns), jnp.bfloat16),
            pltpu.VMEM((levels, vectors, columns), f32),
            pltpu.VMEM((levels, vectors, columns), f32),
            pltpu.VMEM((chunks, outer, 2, 2, rows, LANES), f32),
            pltpu.VMEM((chunks, outer, 2, most, LANES), f32),
            pltpu.VMEM((chunks, outer, 2, most, LANES), f32),
            pltpu.VMEM((chunks, outer, rows, LANES), f32),
            pltpu.VMEM((chunks, outer, rows, LANES), f32),
            pltpu.VMEM((chunks, 2, rows, LANES), f32),
            pltpu.VMEM((chunks, outer, 2, 2, rows, LANES), f32),
            pltpu.VMEM((8, LANES), f32),
            pltpu.VMEM((n, 8, LANES), f32),
            pltpu.VMEM((2, levels, LANES), f32),
            pltpu.VMEM((8, LANES), f32),
            pltpu.VMEM((n, 8, LANES), f32),
            pltpu.VMEM((8, LANES), f32),
            pltpu.VMEM((modes, columns), f32),
            dma((chunks, 8)), dma((chunks, 8)),
            dma((chunks, outer)), dma((chunks, outer)),
            dma((chunks, outer)), dma((chunks, outer)),
            dma((chunks,)), dma((chunks,)),
            dma((n,)), dma((n,)), dma((n,)), dma((n,)),
            dma((1,)), dma((1,)),
        ],
        compiler_params=pltpu.CompilerParams(collective_id=0, has_side_effects=True),
        name="covariance",
    )(perturbations, gradient, horizontal, area.reshape(1, columns), vertical.T)
    return increment, background[0, :vectors]


def solution(mesh):
    return jax.shard_map(
        per_device,
        mesh=mesh,
        in_specs=(
            P(None, "lev", "col"),
            P(None, "lev", "col"),
            P(None, "col"),
            P("col"),
            P(None, "lev"),
        ),
        out_specs=(P(None, "lev", "col"), P()),
        check_vma=False,
    )
```

time: 101 us -> 75.4 us (0.75)
  Pallas kernels: 97.6 us -> 71.1 us
    pallas_call x3 -> x1, Pallas kernels: 97.6 us -> 71.1 us  [per_device(): pl.pallas_call(functools.partial(kernel, sizes, n), out_shape=(jax.ShapeD...]
    unnamed x3 -> x1, local copies, waits for them, and re-layouts: 0.78 us -> 2.31 us
where the time goes in v1:
time: 75.4 us; the launch traced here: 75.2 us
  Pallas kernels  71.1 us (94%)
  local copies, waits for them, and re-layouts  3.5 us (5%)
    pallas_call x1, Pallas kernels, per_device(): pl.pallas_call(functools.partial(kernel, sizes, n), out_shape=(jax.ShapeD...  71.1 us
    unnamed x1, local copies, waits for them, and re-layouts  2.31 us

profile of v1, /device:TPU:0, one launch (start us, length us, event | category | flops | bytes accessed | tf_op | source)
XLA Modules:
  0.0 75.2 jit_solution(11117409340591143883)
XLA Ops:
  0.6 71.1 %covariance.1 = (f32[32,8,1024]{2,1,0:T(8,128)}, f32[8,128]{1,0:T(8,128)}) custom-call(f32[80,8,1024]{2,1,0:T(8,128)} %pert_ref.1, f32[32,8,1024]{2,1,0:T(8,128)} %grad_ref.1, f32[20,1024]{1,0:T(8,128)} %hor_ref.1, f32[1,1024]{1,0:T(1,128)} %bitcast.4, f32[8,20]{1,0:T(8,128)} %bitcast.5), custom_call_target="tpu_custom_call" | custom-call | tf_op jit(solution)/shard_map/covariance/pallas_call | solution.py:432
  71.7 1.2 %slice_bitcast_fusion = f32[32]{0:T(128)} fusion(f32[8,128]{1,0:T(8,128)} %get-tuple-element.5), kind=kLoop, calls=%fused_computation | loop fusion | bytes 256 | tf_op jit(solution)/shard_map/squeeze | solution.py:468
  72.9 2.3 %copy.8 = f32[32,8,1024]{2,1,0:T(8,128)} copy(f32[32,8,1024]{2,1,0:T(8,128)} %get-tuple-element.8) | data formatting | bytes 2097152

commit v2 on v1

--- a/solution.py
+++ b/solution.py
@@ -154,11 +154,15 @@
         for j in range(chunks):
             flat = terms.at[j].reshape(n * rows, LANES)
             flat[used:, :] = jnp.zeros((n * rows - used, LANES), jnp.float32)
-    for l in range(levels):
-        high, low = split(pert_ref[:, l, :])
-        halves[l, :members] = high
-        halves[l, members:] = low
-        weighted[l] = grad_ref[:, l, :] * area
+    for c in range(0, columns, LANES):
+        lanes = slice(c, c + LANES)
+        for k in range(0, members, 16):
+            high, low = split(jnp.swapaxes(pert_ref[k : k + 16, :, lanes], 0, 1))
+            halves[:, k : k + 16, lanes] = high
+            halves[:, members + k : members + k + 16, lanes] = low
+        for v in range(0, vectors, 8):
+            block = jnp.swapaxes(grad_ref[v : v + 8, :, lanes], 0, 1)
+            weighted[:, v : v + 8, lanes] = block * area[:, lanes]
 
     def over_levels(step):
         def body(i, carry):
@@ -302,16 +306,15 @@
                     b = j * group + g
                     term = spread[g * vectors : (g + 1) * vectors] * scaled[b : b + 1, cols]
                     value = term if value is None else value + term
-                if j == chunks - 1:
-                    out_ref[:, l, cols] = value
-                else:
-                    acc[l, :, cols] = value
-
-        if j == chunks - 1:
-            for l in range(levels):
-                step(l)
-        else:
-            over_levels(step)
+                acc[l, :, cols] = value
+
+        over_levels(step)
+
+    def finish_out():
+        for c in range(0, columns, LANES):
+            lanes = slice(c, c + LANES)
+            for v in range(0, vectors, 8):
+                out_ref[v : v + 8, :, lanes] = jnp.swapaxes(acc[:, v : v + 8, lanes], 0, 1)
 
     def take_stats():
         stats[me] = stat_ref[...]
@@ -392,6 +395,7 @@
             send_parts()
         if 0 <= j < chunks:
             forward(j)
+    finish_out()
     take_parts()
 
     for j in range(chunks):
@@ -429,6 +433,8 @@
     vmem = pl.BlockSpec(memory_space=pltpu.VMEM)
     dma = pltpu.SemaphoreType.DMA
 
+    held = chunks * n * rows * LANES * 4 * 9 // 2
+    limit = min(60 * 2**20, held + 14 * 2**20)
     increment, background = pl.pallas_call(
         functools.partial(kernel, sizes, n),
         out_shape=(
@@ -462,7 +468,9 @@
             dma((n,)), dma((n,)), dma((n,)), dma((n,)),
             dma((1,)), dma((1,)),
         ],
-        compiler_params=pltpu.CompilerParams(collective_id=0, has_side_effects=True),
+        compiler_params=pltpu.CompilerParams(
+            collective_id=0, has_side_effects=True, vmem_limit_bytes=limit
+        ),
         name="covariance",
     )(perturbations, gradient, horizontal, area.reshape(1, columns), vertical.T)
     return increment, background[0, :vectors]

time: 75.4 us -> 66.4 us (0.88)
  Pallas kernels: 71.1 us -> 58.8 us
  local copies, waits for them, and re-layouts: 3.5 us -> 6.7 us
    pallas_call x1, Pallas kernels: 71.1 us -> 58.8 us  [per_device(): pl.pallas_call(functools.partial(kernel, sizes, n), out_shape=(jax.ShapeD...]
    unnamed x1 -> x11, local copies, waits for them, and re-layouts: 2.31 us -> 6.19 us
where the time goes in v2:
time: 66.4 us; the launch traced here: 66.1 us
  Pallas kernels  58.8 us (89%)
  local copies, waits for them, and re-layouts  6.7 us (10%)
    pallas_call x1, Pallas kernels, per_device(): pl.pallas_call(functools.partial(kernel, sizes, n), out_shape=(jax.ShapeD...  58.8 us
    unnamed x11, local copies, waits for them, and re-layouts  6.19 us

profile of v2, /device:TPU:0, one launch (start us, length us, event | category | flops | bytes accessed | tf_op | source)
XLA Modules:
  0.0 66.1 jit_solution(10345843458789963239)
XLA Ops:
  0.6 0.0 copy-start
  0.6 1.7 %copy-done = f32[80,8,1024]{2,1,0:T(8,128)S(1)} copy-done((f32[80,8,1024]{2,1,0:T(8,128)S(1)}, f32[80,8,1024]{2,1,0:T(8,128)}, u32[]{:S(2)}) %copy-start) | copy-done | bytes 2621464
  2.4 0.0 copy-start.1
  2.4 1.2 %copy-done.1 = f32[32,8,1024]{2,1,0:T(8,128)S(1)} copy-done((f32[32,8,1024]{2,1,0:T(8,128)S(1)}, f32[32,8,1024]{2,1,0:T(8,128)}, u32[]{:S(2)}) %copy-start.1) | copy-done | bytes 1048600
  3.6 0.0 copy-start.2
  3.6 0.9 %copy-done.2 = f32[20,1024]{1,0:T(8,128)S(1)} copy-done((f32[20,1024]{1,0:T(8,128)S(1)}, f32[20,1024]{1,0:T(8,128)}, u32[]{:S(2)}) %copy-start.2) | copy-done | bytes 81944
  4.5 0.0 copy-start.3
  4.5 0.7 %copy-done.3 = f32[1024]{0:T(1024)S(1)} copy-done((f32[1024]{0:T(1024)S(1)}, f32[1024]{0:T(1024)}, u32[]{:S(2)}) %copy-start.3) | copy-done | bytes 4120
  5.2 0.0 copy-start.4
  5.2 0.7 %copy-done.4 = f32[20,8]{0,1:T(8,128)S(1)} copy-done((f32[20,8]{0,1:T(8,128)S(1)}, f32[20,8]{0,1:T(8,128)}, u32[]{:S(2)}) %copy-start.4) | copy-done | bytes 664
  5.9 58.8 %covariance.1 = (f32[32,8,1024]{2,1,0:T(8,128)S(1)}, f32[8,128]{1,0:T(8,128)S(1)}) custom-call(f32[80,8,1024]{2,1,0:T(8,128)S(1)} %copy-done, f32[32,8,1024]{2,1,0:T(8,128)S(1)} %copy-done.1, f32[20,1024]{1,0:T(8,128)S(1)} %copy-done.2, f32[1,1024]{1,0:T(1,128)S(1)} %bitcast.4, f32[8,20]{1,0:T(8,128)S(1)} %bitcast.5), custom_call_target="tpu_custom_call" | custom-call | tf_op jit(solution)/shard_map/covariance/pallas_call | solution.py:438
  64.6 0.5 slice_bitcast_fusion
  65.2 1.0 %copy.8 = f32[32,8,1024]{2,1,0:T(8,128)} copy(f32[32,8,1024]{2,1,0:T(8,128)S(1)} %get-tuple-element.8) | data formatting | bytes 2097152
Async XLA Ops:
  0.6 1.7 %copy-start = (f32[80,8,1024]{2,1,0:T(8,128)S(1)}, f32[80,8,1024]{2,1,0:T(8,128)}, u32[]{:S(2)}) copy-start(f32[80,8,1024]{2,1,0:T(8,128)} %pert_ref.1) | copy-start | bytes 7864324
  2.4 1.2 %copy-start.1 = (f32[32,8,1024]{2,1,0:T(8,128)S(1)}, f32[32,8,1024]{2,1,0:T(8,128)}, u32[]{:S(2)}) copy-start(f32[32,8,1024]{2,1,0:T(8,128)} %grad_ref.1) | copy-start | bytes 3145732
  3.6 0.9 %copy-start.2 = (f32[20,1024]{1,0:T(8,128)S(1)}, f32[20,1024]{1,0:T(8,128)}, u32[]{:S(2)}) copy-start(f32[20,1024]{1,0:T(8,128)} %hor_ref.1) | copy-start | bytes 245764
  4.5 0.7 %copy-start.3 = (f32[1024]{0:T(1024)S(1)}, f32[1024]{0:T(1024)}, u32[]{:S(2)}) copy-start(f32[1024]{0:T(1024)} %param.8) | copy-start | bytes 12292
  5.2 0.7 %copy-start.4 = (f32[20,8]{0,1:T(8,128)S(1)}, f32[20,8]{0,1:T(8,128)}, u32[]{:S(2)}) copy-start(f32[20,8]{0,1:T(8,128)} %param.9) | copy-start | bytes 1924

commit v3 on v2

v3 whole, which is shorter than its diff:
```python
import functools

import jax
import jax.numpy as jnp
from jax import lax
from jax.experimental import pallas as pl
from jax.experimental.pallas import tpu as pltpu
from jax.sharding import PartitionSpec as P

LANES = 128
NT = (((1,), (1,)), ((), ()))
TN = (((0,), (0,)), ((), ()))
NN = (((1,), (0,)), ((), ()))
UNROLL = 2
BLOCKS = 4


def split(x):
    high = x.astype(jnp.bfloat16)
    low = (x - high.astype(jnp.float32)).astype(jnp.bfloat16)
    return high, low


def exact_dot(a, b, dims):
    return lax.dot_general(
        a, b, dims, precision=lax.Precision.HIGHEST, preferred_element_type=jnp.float32
    )


def timetable(*stages):
    starts = (3.5, 8.3, 12.8, 17.0, 22.9, 29.1, 32.5, 40.7)
    paces = (2.05, 2.4, 2.7, 2.6, 2.9, 2.9, 3.0, 2.3)
    return zip(stages, starts, paces)


def kernel(
    sizes, n, pert_hbm, grad_hbm, hor_hbm, area_hbm, vert_hbm, out_ref, bg_ref,
    pert_ref, grad_ref, hor_ref, area_ref, vert_ref,
    halves, weighted, acc, terms, first_a, first_b, second, third, raised, lifted,
    totals, verticals, sums, weights, scaled,
    load_p, load_s, send_h, recv_h, send_g, recv_g, send_l, recv_l, send_m, recv_m,
    send_t, recv_t, send_v, recv_v,
):
    members, levels, vectors, modes, columns = sizes
    group = LANES // vectors
    chunks = modes // group
    vmodes = vert_ref.shape[1]
    rows = terms.shape[4]
    tiles = rows // levels
    outer = n // 4
    used = members * levels
    me = lax.axis_index("col")
    lev = lax.axis_index("lev")
    other = 1 - lev
    x = lax.rem(me, 2)
    y = lax.rem(lax.div(me, 2), 2)
    h = lax.div(me, 4)
    not_x, not_y = 1 - x, 1 - y
    x_peer = (4 * h + 2 * y + not_x, lev)
    y_peer = (4 * h + 2 * not_y + x, lev)
    partner = (me, other)
    mesh_id = pl.DeviceIdType.MESH
    barrier = pltpu.get_barrier_semaphore()

    def along(p):
        return 4 * lax.rem(h + p, outer) + 2 * y + x

    def greet(device):
        pl.semaphore_signal(barrier, inc=1, device_id=device, device_id_type=mesh_id)

    def greet_outer(p, carry):
        greet((along(p), lev))
        greet((along(p), other))
        return carry

    for device in (x_peer, y_peer, partner):
        greet(device)
    lax.fori_loop(1, outer, greet_outer, 0)

    wide_block = columns // BLOCKS

    def load_block(q):
        part = pl.ds(q * wide_block, wide_block)
        return (
            pltpu.make_async_copy(
                pert_hbm.at[:, :, part], pert_ref.at[:, :, part], load_p.at[0, q]
            ),
            pltpu.make_async_copy(
                grad_hbm.at[:, :, part], grad_ref.at[:, :, part], load_p.at[1, q]
            ),
        )

    small = [
        pltpu.make_async_copy(source, target, load_s.at[i])
        for i, (source, target) in enumerate(
            ((area_hbm, area_ref), (hor_hbm, hor_ref), (vert_hbm, vert_ref))
        )
    ]
    for copy in small:
        copy.start()
    for q in range(BLOCKS):
        for copy in load_block(q):
            copy.start()

    def remote(src, dst, send, recv, device):
        return pltpu.make_async_remote_copy(
            src_ref=src, dst_ref=dst, send_sem=send, recv_sem=recv,
            device_id=device, device_id_type=mesh_id,
        )

    def halfway(j):
        count = (tiles + 1 - j % 2) // 2 * levels
        return pl.ds(0, count), pl.ds(count, rows - count), count, rows - count

    def half_copy(j, i, src, dst, device):
        return remote(src, dst, send_h.at[j, i], recv_h.at[j, i], device)

    def one(j):
        a, b, na, nb = halfway(j)
        return (
            half_copy(j, 0, terms.at[j, :, :, not_x, a], first_a.at[j, :, :, pl.ds(0, na)], x_peer),
            half_copy(j, 1, terms.at[j, :, not_y, :, b], first_b.at[j, :, :, pl.ds(0, nb)], y_peer),
        )

    def two(j):
        a, b, na, nb = halfway(j)
        return (
            half_copy(j, 2, first_a.at[j, :, not_y, pl.ds(0, na)], second.at[j, :, a], y_peer),
            half_copy(j, 3, first_b.at[j, :, not_x, pl.ds(0, nb)], second.at[j, :, b], x_peer),
        )

    def keeper(j):
        return j % 2

    def outer_copy(j, p, source):
        return remote(
            second.at[j, lax.rem(h + p, outer)], third.at[j, source, p],
            send_g.at[j, p], recv_g.at[j, source, p], (along(p), keeper(j)),
        )

    def lifted_copy(j, p, slot):
        block = lifted.at[j, slot, y, x]
        return remote(block, block, send_l.at[j, p], recv_l.at[j, p], (along(p), lev))

    def raised_copy(j, p, slot):
        return remote(
            raised.at[j], lifted.at[j, slot, y, x],
            send_m.at[j, p], recv_m.at[j, p], (along(p), other),
        )

    def three(j, yy, xx):
        a, b, _, _ = halfway(j)
        block_a = lifted.at[j, :, yy, x, a]
        block_b = lifted.at[j, :, y, xx, b]
        return (
            half_copy(j, 4, block_a, block_a, y_peer),
            half_copy(j, 5, block_b, block_b, x_peer),
        )

    def four(j, yy, xx):
        a, b, _, _ = halfway(j)
        block_a = lifted.at[j, :, :, xx, a]
        block_b = lifted.at[j, :, yy, :, b]
        return (
            half_copy(j, 6, block_a, block_a, x_peer),
            half_copy(j, 7, block_b, block_b, y_peer),
        )

    def vert_copy(slot):
        block = verticals.at[slot]
        return remote(block, block, send_v.at[0], recv_v.at[0], partner)

    def total_copy(k, source, target, device):
        return remote(
            totals.at[k, source], totals.at[k, target],
            send_t.at[k, target], recv_t.at[k, target], device,
        )

    def total_outer(k, p):
        return total_copy(k, 6, 6 + p, (along(p), lev))

    def total_x(k):
        return total_copy(k, 0, 1, x_peer)

    def total_y(k):
        return total_copy(k, 2, 3, y_peer)

    def total_c(k):
        return total_copy(k, 4, 5, partner)

    def send_total_x(k):
        total_x(k).start()

    def send_total_y(k):
        total_x(k).wait_recv()
        totals[k, 2] = totals[k, 0] + totals[k, 1]
        total_y(k).start()

    def send_total_c(k):
        total_y(k).wait_recv()
        totals[k, 4] = totals[k, 2] + totals[k, 3]
        total_c(k).start()

    def send_total_outer(k):
        total_c(k).wait_recv()
        totals[k, 6] = totals[k, 4] + totals[k, 5]

        def send(p, carry):
            total_outer(k, p).start()
            return carry

        lax.fori_loop(1, outer, send, 0)

    def take_total(k):
        def take(p, carry):
            total_outer(k, p).wait_recv()
            return carry + totals[k, 6 + p]

        return lax.fori_loop(1, outer, take, totals[k, 6])

    lane = lax.broadcasted_iota(jnp.int32, (modes, LANES), 1)
    row = lax.broadcasted_iota(jnp.int32, (modes, LANES), 0)
    sums[...] = jnp.zeros(sums.shape, jnp.float32)
    verticals[lev] = jnp.zeros(verticals.shape[1:], jnp.float32)
    if used < n * rows:
        for j in range(chunks):
            flat = terms.at[j].reshape(n * rows, LANES)
            flat[used:, :] = jnp.zeros((n * rows - used, LANES), jnp.float32)
    for copy in small:
        copy.wait()
    area = area_ref[...]
    verticals[lev, :, :vmodes] = vert_ref[...]

    def prepare():
        for q in range(BLOCKS):
            for copy in load_block(q):
                copy.wait()
            for c in range(q * wide_block, (q + 1) * wide_block, LANES):
                lanes = slice(c, c + LANES)
                for k in range(0, members, 16):
                    high, low = split(jnp.swapaxes(pert_ref[k : k + 16, :, lanes], 0, 1))
                    halves[:, k : k + 16, lanes] = high
                    halves[:, members + k : members + k + 16, lanes] = low
                for v in range(0, vectors, 8):
                    block = jnp.swapaxes(grad_ref[v : v + 8, :, lanes], 0, 1)
                    weighted[:, v : v + 8, lanes] = block * area[:, lanes]

    def statistics():
        power = jnp.sum(area * hor_ref[...] * hor_ref[...], axis=1, keepdims=True)
        powers = jnp.sum(
            jnp.where(lane == row, jnp.broadcast_to(power, (modes, LANES)), 0.0),
            axis=0, keepdims=True,
        )
        total = jnp.broadcast_to(jnp.sum(area, axis=1, keepdims=True), (1, LANES))
        stat_row = jnp.where(lane[:1] == modes, total, powers)
        totals[0, 0] = jnp.broadcast_to(stat_row, totals.shape[2:])

    def over_levels(step):
        def body(i, carry):
            for u in range(UNROLL):
                step(i * UNROLL + u)
            return carry

        lax.fori_loop(0, levels // UNROLL, body, 0)

    def adjoint(j):
        flat = terms.at[j].reshape(n * rows, LANES)

        def step(l):
            base = weighted[l]
            products = jnp.concatenate(
                [base * hor_ref[b : b + 1, :] for b in range(j * group, (j + 1) * group)],
                axis=0,
            )
            both = jnp.concatenate(split(products), axis=0)
            out = lax.dot_general(halves[l], both, NT, preferred_element_type=jnp.float32)
            flat[pl.ds(l, members, stride=levels), :] = out[:members, :LANES] + (
                out[members:, :LANES] + out[:members, LANES:]
            )

        over_levels(step)

    def send_one(j):
        for copy in one(j):
            copy.start()

    def send_two(j):
        a, b, na, nb = halfway(j)
        one_a, one_b = one(j)
        two_a, two_b = two(j)

        def add_a(i, carry):
            first_a[j, i, not_y, :na] += terms[j, i, not_y, x, a]
            return carry

        def add_b(i, carry):
            first_b[j, i, not_x, :nb] += terms[j, i, y, not_x, b]
            return carry

        one_a.wait_recv()
        lax.fori_loop(0, outer, add_a, 0)
        two_a.start()
        one_b.wait_recv()
        lax.fori_loop(0, outer, add_b, 0)
        two_b.start()

    def add_second(j, there):
        a, b, na, nb = halfway(j)
        second[j, there, a] += terms[j, there, y, x, a] + first_a[j, there, y, :na]
        second[j, there, b] += terms[j, there, y, x, b] + first_b[j, there, x, :nb]

    def send_three(j):
        for copy in two(j):
            copy.wait_recv()

        def send_outer(p, carry):
            add_second(j, lax.rem(h + p, outer))
            outer_copy(j, p, lev).start()
            return carry

        lax.fori_loop(1, outer, send_outer, 0)
        add_second(j, h)

        @pl.when(lev != keeper(j))
        def _():
            outer_copy(j, 0, lev).start()

    def mix(j):
        @pl.when(lev == keeper(j))
        def _():
            def take(p, carry):
                outer_copy(j, p, lev).wait_recv()
                second[j, h] += third[j, lev, p]
                outer_copy(j, p, other).wait_recv()
                third[j, other, 0] += third[j, other, p]
                return carry

            outer_copy(j, 0, other).wait_recv()
            lax.fori_loop(1, outer, take, 0)

            def wide(block):
                return jnp.concatenate(
                    [block[i * levels : (i + 1) * levels] for i in range(tiles)], axis=1
                )

            far = verticals[other][:, :vmodes]
            control = exact_dot(vert_ref[...], wide(second[j, h]), TN) + exact_dot(
                far, wide(third[j, other, 0]), TN
            )
            near_lifted = exact_dot(vert_ref[...], control, NN)
            far_lifted = exact_dot(far, control, NN)
            square = jnp.zeros((1, LANES), jnp.float32)
            for i in range(tiles):
                lanes = slice(i * LANES, (i + 1) * LANES)
                part = slice(i * levels, (i + 1) * levels)
                lifted[j, h, y, x, part, :] = near_lifted[:, lanes]
                raised[j, part, :] = far_lifted[:, lanes]
                square = square + jnp.sum(
                    control[:, lanes] * control[:, lanes], axis=0, keepdims=True
                )
            sums[j : j + 1, :] = square

            def start_lifted(p, carry):
                lifted_copy(j, p, h).start()
                raised_copy(j, p, h).start()
                return carry

            raised_copy(j, 0, h).start()
            lax.fori_loop(1, outer, start_lifted, 0)

    def send_g2(j):
        @pl.when(lev == keeper(j))
        def _():
            def take(p, carry):
                lifted_copy(j, p, lax.rem(h + outer - p, outer)).wait_recv()
                return carry

            lax.fori_loop(1, outer, take, 0)

        @pl.when(lev != keeper(j))
        def _():
            def take(p, carry):
                raised_copy(j, p, lax.rem(h + outer - p, outer)).wait_recv()
                return carry

            lax.fori_loop(0, outer, take, 0)

        for copy in three(j, y, x):
            copy.start()

    def send_g3(j):
        three_a, three_b = three(j, not_y, not_x)
        four_a, four_b = four(j, y, x)
        three_a.wait_recv()
        four_a.start()
        three_b.wait_recv()
        four_b.start()

    def forward(j):
        for copy in four(j, not_y, not_x):
            copy.wait_recv()
        flat = lifted.at[j].reshape(n * rows, LANES)
        width = 256

        def step(l):
            high, low = split(flat[pl.ds(l, members, stride=levels), :])
            lhs = jnp.concatenate([high, high, low], axis=0)
            for c in range(0, columns, width):
                cols = slice(c, c + width)
                rhs = jnp.concatenate([halves[l, :, cols], halves[l, :members, cols]], axis=0)
                spread = lax.dot_general(lhs, rhs, TN, preferred_element_type=jnp.float32)
                value = None if j == 0 else acc[l, :, cols]
                for g in range(group):
                    b = j * group + g
                    term = spread[g * vectors : (g + 1) * vectors] * scaled[b : b + 1, cols]
                    value = term if value is None else value + term
                acc[l, :, cols] = value

        over_levels(step)

    def take_stats(k):
        stat = 0.5 * take_total(k)
        spread = jnp.broadcast_to(stat[:1], (modes, LANES))
        power = jnp.sum(jnp.where(lane == row, spread, 0.0), axis=1, keepdims=True)
        whole = jnp.sum(jnp.where(lane == modes, spread, 0.0), axis=1, keepdims=True)
        factor = 1.0 / jnp.sqrt(modes * (power / whole + 1e-06))
        scale = factor * (columns * n / whole)
        scaled[...] = hor_ref[...] * (factor * scale)
        placed = jnp.where(
            lax.div(lane, vectors) == lax.rem(row, group),
            jnp.broadcast_to(scale, lane.shape), 0.0,
        )
        for j in range(chunks):
            weights[j : j + 1, :] = jnp.sum(
                placed[j * group : (j + 1) * group], axis=0, keepdims=True
            )

    def gather_sums(k):
        part = jnp.zeros((1, LANES), jnp.float32)
        for j in range(chunks):
            weight = weights[j : j + 1, :]
            part = part + sums[j : j + 1, :] * weight * weight
        totals[k, 0] = jnp.broadcast_to(part, totals.shape[2:])
        send_total_x(k)

    def finish_sums(k):
        part = take_total(k)
        folded = part
        for g in range(1, group):
            folded = folded + pltpu.roll(part, g * vectors, 1)
        bg_ref[...] = 0.5 * folded

    def meet(k):
        pl.semaphore_wait(barrier, 3 + 2 * (outer - 1))
        vert_copy(lev).start()

    def take_vert(k):
        vert_copy(other).wait_recv()

    def set_stats(k):
        statistics()
        send_total_x(k)

    def finish_out(k):
        for c in range(0, columns, LANES):
            lanes = slice(c, c + LANES)
            for v in range(0, vectors, 8):
                out_ref[v : v + 8, :, lanes] = jnp.swapaxes(acc[:, v : v + 8, lanes], 0, 1)

    plan = [
        (start + pace * j, stage, j)
        for stage, start, pace in timetable(
            adjoint, send_one, send_two, send_three, mix, send_g2, send_g3, forward
        )
        for j in range(chunks)
    ]
    last = chunks - 5
    plan += [
        (8.2, meet, 0), (8.65, set_stats, 0), (13.0, send_total_y, 0), (16.7, send_total_c, 0),
        (19.0, send_total_outer, 0), (20.0, take_vert, 0), (26.0, take_stats, 0),
        (36.0 + 3 * last, gather_sums, 1), (38.85 + 3 * last, send_total_y, 1),
        (41.5 + 3 * last, send_total_c, 1), (43.5 + 3 * last, send_total_outer, 1),
        (1000.0, finish_out, 0), (1001.0, finish_sums, 1),
    ]
    prepare()
    for _, stage, j in sorted(plan, key=lambda entry: entry[0]):
        stage(j)

    for j in range(chunks):
        for copy in one(j) + two(j) + three(j, y, x) + four(j, y, x):
            copy.wait_send()

        def sent_outer(p, carry):
            outer_copy(j, p, lev).wait_send()
            return carry

        lax.fori_loop(1, outer, sent_outer, 0)

        @pl.when(lev != keeper(j))
        def _():
            outer_copy(j, 0, lev).wait_send()

        @pl.when(lev == keeper(j))
        def _():
            def sent(p, carry):
                lifted_copy(j, p, h).wait_send()
                raised_copy(j, p, h).wait_send()
                return carry

            raised_copy(j, 0, h).wait_send()
            lax.fori_loop(1, outer, sent, 0)

    for k in range(2):
        for copy in (total_x(k), total_y(k), total_c(k)):
            copy.wait_send()

        def sent_total(p, carry):
            total_outer(k, p).wait_send()
            return carry

        lax.fori_loop(1, outer, sent_total, 0)
    vert_copy(lev).wait_send()


def per_device(perturbations, gradient, horizontal, area, vertical):
    members, levels, columns = perturbations.shape
    vectors = gradient.shape[0]
    modes = horizontal.shape[0]
    n = lax.axis_size("col")
    sizes = (members, levels, vectors, modes, columns)
    chunks = modes * vectors // LANES
    tiles = max(2, -(-members // n))
    rows = tiles * levels
    outer = n // 4
    most = (tiles + 1) // 2 * levels
    f32 = jnp.float32
    vmem = pl.BlockSpec(memory_space=pltpu.VMEM)
    dma = pltpu.SemaphoreType.DMA

    held = chunks * n * rows * LANES * 4 * 9 // 2
    limit = min(60 * 2**20, held + 20 * 2**20)
    increment, background = pl.pallas_call(
        functools.partial(kernel, sizes, n),
        out_shape=(
            jax.ShapeDtypeStruct((vectors, levels, columns), f32),
            jax.ShapeDtypeStruct((8, LANES), f32),
        ),
        in_specs=[pl.BlockSpec(memory_space=pltpu.HBM)] * 5,
        out_specs=(vmem, vmem),
        scratch_shapes=[
            pltpu.VMEM((members, levels, columns), f32),
            pltpu.VMEM((vectors, levels, columns), f32),
            pltpu.VMEM((modes, columns), f32),
            pltpu.VMEM((1, columns), f32),
            pltpu.VMEM((levels, vertical.shape[0]), f32),
            pltpu.VMEM((levels, 2 * members, columns), jnp.bfloat16),
            pltpu.VMEM((levels, vectors, columns), f32),
            pltpu.VMEM((levels, vectors, columns), f32),
            pltpu.VMEM((chunks, outer, 2, 2, rows, LANES), f32),
            pltpu.VMEM((chunks, outer, 2, most, LANES), f32),
            pltpu.VMEM((chunks, outer, 2, most, LANES), f32),
            pltpu.VMEM((chunks, outer, rows, LANES), f32),
            pltpu.VMEM((chunks, 2, outer, rows, LANES), f32),
            pltpu.VMEM((chunks, rows, LANES), f32),
            pltpu.VMEM((chunks, outer, 2, 2, rows, LANES), f32),
            pltpu.VMEM((2, 6 + outer, 8, LANES), f32),
            pltpu.VMEM((2, levels, LANES), f32),
            pltpu.VMEM((8, LANES), f32),
            pltpu.VMEM((8, LANES), f32),
            pltpu.VMEM((modes, columns), f32),
            dma((2, BLOCKS)), dma((3,)),
            dma((chunks, 8)), dma((chunks, 8)),
            dma((chunks, outer)), dma((chunks, 2, outer)),
            dma((chunks, outer)), dma((chunks, outer)),
            dma((chunks, outer)), dma((chunks, outer)),
            dma((2, 6 + outer)), dma((2, 6 + outer)),
            dma((1,)), dma((1,)),
        ],
        compiler_params=pltpu.CompilerParams(
            collective_id=0, has_side_effects=True, vmem_limit_bytes=limit
        ),
        name="covariance",
    )(*(
        pltpu.with_memory_space_constraint(array, pltpu.HBM)
        for array in (perturbations, gradient, horizontal, area.reshape(1, columns), vertical.T)
    ))
    return increment, background[0, :vectors]


def solution(mesh):
    return jax.shard_map(
        per_device,
        mesh=mesh,
        in_specs=(
            P(None, "lev", "col"),
            P(None, "lev", "col"),
            P(None, "col"),
            P("col"),
            P(None, "lev"),
        ),
        out_specs=(P(None, "lev", "col"), P()),
        check_vma=False,
    )
```

time: 66.4 us -> 58.5 us (0.88)
  local copies, waits for them, and re-layouts: 6.7 us -> 1.48 us
  Pallas kernels: 58.8 us -> 56.2 us
    unnamed x11 -> x1, local copies, waits for them, and re-layouts: 6.19 us -> 0.97 us
    pallas_call x1, Pallas kernels: 58.8 us -> 56.2 us  [per_device(): pl.pallas_call(functools.partial(kernel, sizes, n), out_shape=(jax.ShapeD...]
where the time goes in v3:
time: 58.5 us; the launch traced here: 58.3 us
  Pallas kernels  56.2 us (96%)
  local copies, waits for them, and re-layouts  1.48 us (3%)
  between operations  0.64 us (1%)
    pallas_call x1, Pallas kernels, per_device(): pl.pallas_call(functools.partial(kernel, sizes, n), out_shape=(jax.ShapeD...  56.2 us

profile of v3, /device:TPU:0, one launch (start us, length us, event | category | flops | bytes accessed | tf_op | source)
XLA Modules:
  0.0 58.3 jit_solution(3360887569415500914)
XLA Ops:
  0.6 56.2 %covariance.1 = (f32[32,8,1024]{2,1,0:T(8,128)S(1)}, f32[8,128]{1,0:T(8,128)S(1)}) custom-call(f32[80,8,1024]{2,1,0:T(8,128)} %pert_hbm.1, f32[32,8,1024]{2,1,0:T(8,128)} %grad_hbm.1, f32[20,1024]{1,0:T(8,128)} %hor_hbm.1, f32[1,1024]{1,0:T(1,128)} %bitcast.4, f32[8,20]{1,0:T(8,128)} %bitcast.5), custom_call_target="tpu_custom_call" | custom-call | tf_op jit(solution)/shard_map/covariance/pallas_call | solution.py:542
  56.9 0.5 slice_bitcast_fusion
  57.4 1.0 %copy.8 = f32[32,8,1024]{2,1,0:T(8,128)} copy(f32[32,8,1024]{2,1,0:T(8,128)S(1)} %get-tuple-element.8) | data formatting | bytes 2097152

commit v4 on v3

--- a/solution.py
+++ b/solution.py
@@ -11,7 +11,7 @@
 NT = (((1,), (1,)), ((), ()))
 TN = (((0,), (0,)), ((), ()))
 NN = (((1,), (0,)), ((), ()))
-UNROLL = 2
+UNROLL = 8
 BLOCKS = 4
 
 
@@ -37,7 +37,7 @@
     sizes, n, pert_hbm, grad_hbm, hor_hbm, area_hbm, vert_hbm, out_ref, bg_ref,
     pert_ref, grad_ref, hor_ref, area_ref, vert_ref,
     halves, weighted, acc, terms, first_a, first_b, second, third, raised, lifted,
-    totals, verticals, sums, weights, scaled,
+    near, far_z, plane_a, plane_b, totals, verticals, sums, weights, scaled,
     load_p, load_s, send_h, recv_h, send_g, recv_g, send_l, recv_l, send_m, recv_m,
     send_t, recv_t, send_v, recv_v,
 ):
@@ -132,6 +132,70 @@
     def keeper(j):
         return j % 2
 
+    z_first = outer == 4
+    low_bit, high_bit = lax.rem(h, 2), lax.div(h, 2)
+    z_near = (4 * (2 * high_bit + 1 - low_bit) + 2 * y + x, lev)
+    z_far = (4 * (2 * (1 - high_bit) + low_bit) + 2 * y + x, lev)
+
+    def paired(ref):
+        return ref.at[0].reshape(2, 2, 2, 2, rows, LANES)
+
+    def near_copy():
+        return half_copy(0, 0, paired(terms).at[:, 1 - low_bit], near, z_near)
+
+    def far_copy():
+        return half_copy(0, 1, near.at[1 - high_bit], far_z, z_far)
+
+    def plane_one():
+        a, b, na, nb = halfway(0)
+        return (
+            half_copy(0, 2, far_z.at[:, not_x, a], plane_a, x_peer),
+            half_copy(0, 3, far_z.at[not_y, :, b], plane_b, y_peer),
+        )
+
+    def plane_two():
+        a, b, na, nb = halfway(0)
+        return (
+            half_copy(0, 4, plane_a.at[not_y], second.at[0, 0, a], y_peer),
+            half_copy(0, 5, plane_b.at[not_x], second.at[0, 0, b], x_peer),
+        )
+
+    def own_copy():
+        return remote(
+            second.at[0, 0], third.at[0, lev, 0], send_g.at[0, 0], recv_g.at[0, lev, 0], partner
+        )
+
+    def own_arrival():
+        return remote(
+            second.at[0, 0], third.at[0, other, 0], send_g.at[0, 0], recv_g.at[0, other, 0], partner
+        )
+
+    def back_one(yy, xx):
+        a, b, _, _ = halfway(0)
+        block_a = lifted.at[0, h, yy, x, a]
+        block_b = lifted.at[0, h, y, xx, b]
+        return (
+            half_copy(0, 6, block_a, block_a, y_peer),
+            half_copy(0, 7, block_b, block_b, x_peer),
+        )
+
+    def back_two(yy, xx):
+        a, b, _, _ = halfway(0)
+        block_a = lifted.at[0, h, :, xx, a]
+        block_b = lifted.at[0, h, yy, :, b]
+        return (
+            half_copy(0, 8, block_a, block_a, x_peer),
+            half_copy(0, 9, block_b, block_b, y_peer),
+        )
+
+    def back_far(slot):
+        block = lifted.at[0, slot]
+        return half_copy(0, 10, block, block, z_far)
+
+    def back_near(bit):
+        block = paired(lifted).at[:, bit]
+        return half_copy(0, 11, block, block, z_near)
+
     def outer_copy(j, p, source):
         return remote(
             second.at[j, lax.rem(h + p, outer)], third.at[j, source, p],
@@ -304,6 +368,70 @@
         lax.fori_loop(0, outer, add_b, 0)
         two_b.start()
 
+    def z_start(j):
+        near_copy().start()
+
+    def z_middle(j):
+        near_copy().wait_recv()
+        mine = paired(terms)
+        for i in range(2):
+            near[i] += mine[i, low_bit]
+        far_copy().start()
+
+    def z_end(j):
+        a, b, na, nb = halfway(0)
+        far_copy().wait_recv()
+        far_z[...] += near[high_bit]
+        for copy in plane_one():
+            copy.start()
+
+    def z_plane(j):
+        a, b, na, nb = halfway(0)
+        one_a, one_b = plane_one()
+        two_a, two_b = plane_two()
+        one_a.wait_recv()
+        plane_a[not_y] += far_z[not_y, x, a]
+        two_a.start()
+        one_b.wait_recv()
+        plane_b[not_x] += far_z[y, not_x, b]
+        two_b.start()
+
+    def z_own(j):
+        a, b, na, nb = halfway(0)
+        for copy in plane_two():
+            copy.wait_recv()
+        second[0, 0, a] += far_z[y, x, a] + plane_a[y]
+        second[0, 0, b] += far_z[y, x, b] + plane_b[x]
+
+        @pl.when(lev != keeper(0))
+        def _():
+            own_copy().start()
+
+    def z_back(j):
+        @pl.when(lev != keeper(0))
+        def _():
+            raised_copy(0, 0, h).wait_recv()
+
+        for copy in back_one(y, x):
+            copy.start()
+
+    def z_back_plane(j):
+        one_a, one_b = back_one(not_y, not_x)
+        two_a, two_b = back_two(y, x)
+        one_a.wait_recv()
+        two_a.start()
+        one_b.wait_recv()
+        two_b.start()
+
+    def z_back_far(j):
+        for copy in back_two(not_y, not_x):
+            copy.wait_recv()
+        back_far(h).start()
+
+    def z_back_near(j):
+        back_far(2 * (1 - high_bit) + low_bit).wait_recv()
+        back_near(low_bit).start()
+
     def add_second(j, there):
         a, b, na, nb = halfway(j)
         second[j, there, a] += terms[j, there, y, x, a] + first_a[j, there, y, :na]
@@ -328,6 +456,9 @@
     def mix(j):
         @pl.when(lev == keeper(j))
         def _():
+            direct = z_first and j == 0
+            mine = 0 if direct else h
+
             def take(p, carry):
                 outer_copy(j, p, lev).wait_recv()
                 second[j, h] += third[j, lev, p]
@@ -335,8 +466,11 @@
                 third[j, other, 0] += third[j, other, p]
                 return carry
 
-            outer_copy(j, 0, other).wait_recv()
-            lax.fori_loop(1, outer, take, 0)
+            if direct:
+                own_arrival().wait_recv()
+            else:
+                outer_copy(j, 0, other).wait_recv()
+                lax.fori_loop(1, outer, take, 0)
 
             def wide(block):
                 return jnp.concatenate(
@@ -344,7 +478,7 @@
                 )
 
             far = verticals[other][:, :vmodes]
-            control = exact_dot(vert_ref[...], wide(second[j, h]), TN) + exact_dot(
+            control = exact_dot(vert_ref[...], wide(second[j, mine]), TN) + exact_dot(
                 far, wide(third[j, other, 0]), TN
             )
             near_lifted = exact_dot(vert_ref[...], control, NN)
@@ -366,7 +500,8 @@
                 return carry
 
             raised_copy(j, 0, h).start()
-            lax.fori_loop(1, outer, start_lifted, 0)
+            if not direct:
+                lax.fori_loop(1, outer, start_lifted, 0)
 
     def send_g2(j):
         @pl.when(lev == keeper(j))
@@ -397,8 +532,11 @@
         four_b.start()
 
     def forward(j):
-        for copy in four(j, not_y, not_x):
-            copy.wait_recv()
+        if z_first and j == 0:
+            back_near(1 - low_bit).wait_recv()
+        else:
+            for copy in four(j, not_y, not_x):
+                copy.wait_recv()
         flat = lifted.at[j].reshape(n * rows, LANES)
         width = 256
 
@@ -467,16 +605,22 @@
             for v in range(0, vectors, 8):
                 out_ref[v : v + 8, :, lanes] = jnp.swapaxes(acc[:, v : v + 8, lanes], 0, 1)
 
-    plan = [
-        (start + pace * j, stage, j)
-        for stage, start, pace in timetable(
-            adjoint, send_one, send_two, send_three, mix, send_g2, send_g3, forward
-        )
-        for j in range(chunks)
-    ]
+    shift = 1 if z_first else 0
+    plan = []
+    for index, (stage, start, pace) in enumerate(
+        timetable(adjoint, send_one, send_two, send_three, mix, send_g2, send_g3, forward)
+    ):
+        for j in range(0 if index in (0, 7) else shift, chunks):
+            plan.append((start + pace * (j if index in (0, 7) else j - shift), stage, j))
+    if z_first:
+        plan += [
+            (6.9, z_start, 0), (12.5, z_middle, 0), (16.8, z_end, 0), (18.5, z_plane, 0),
+            (20.5, z_own, 0), (22.5, mix, 0), (24.5, z_back, 0), (26.5, z_back_plane, 0),
+            (28.5, z_back_far, 0), (32.4, z_back_near, 0),
+        ]
     last = chunks - 5
     plan += [
-        (8.2, meet, 0), (8.65, set_stats, 0), (13.0, send_total_y, 0), (16.7, send_total_c, 0),
+        (6.8, meet, 0), (8.65, set_stats, 0), (13.0, send_total_y, 0), (16.7, send_total_c, 0),
         (19.0, send_total_outer, 0), (20.0, take_vert, 0), (26.0, take_stats, 0),
         (36.0 + 3 * last, gather_sums, 1), (38.85 + 3 * last, send_total_y, 1),
         (41.5 + 3 * last, send_total_c, 1), (43.5 + 3 * last, send_total_outer, 1),
@@ -486,7 +630,22 @@
     for _, stage, j in sorted(plan, key=lambda entry: entry[0]):
         stage(j)
 
-    for j in range(chunks):
+    if z_first:
+        for copy in (
+            (near_copy(), far_copy(), back_far(h), back_near(low_bit))
+            + plane_one() + plane_two() + back_one(y, x) + back_two(y, x)
+        ):
+            copy.wait_send()
+
+        @pl.when(lev != keeper(0))
+        def _():
+            own_copy().wait_send()
+
+        @pl.when(lev == keeper(0))
+        def _():
+            raised_copy(0, 0, h).wait_send()
+
+    for j in range(shift, chunks):
         for copy in one(j) + two(j) + three(j, y, x) + four(j, y, x):
             copy.wait_send()
 
@@ -563,13 +722,17 @@
             pltpu.VMEM((chunks, 2, outer, rows, LANES), f32),
             pltpu.VMEM((chunks, rows, LANES), f32),
             pltpu.VMEM((chunks, outer, 2, 2, rows, LANES), f32),
+            pltpu.VMEM((2, 2, 2, rows, LANES), f32),
+            pltpu.VMEM((2, 2, rows, LANES), f32),
+            pltpu.VMEM((2, most, LANES), f32),
+            pltpu.VMEM((2, rows - most, LANES), f32),
             pltpu.VMEM((2, 6 + outer, 8, LANES), f32),
             pltpu.VMEM((2, levels, LANES), f32),
             pltpu.VMEM((8, LANES), f32),
             pltpu.VMEM((8, LANES), f32),
             pltpu.VMEM((modes, columns), f32),
             dma((2, BLOCKS)), dma((3,)),
-            dma((chunks, 8)), dma((chunks, 8)),
+            dma((chunks, 12)), dma((chunks, 12)),
             dma((chunks, outer)), dma((chunks, 2, outer)),
             dma((chunks, outer)), dma((chunks, outer)),
             dma((chunks, outer)), dma((chunks, outer)),

time: 58.5 us -> 59.2 us (1.012)
  Pallas kernels: 56.2 us -> 56.9 us
    pallas_call x1, Pallas kernels: 56.2 us -> 56.9 us  [per_device(): pl.pallas_call(functools.partial(kernel, sizes, n), out_shape=(jax.ShapeD...]
where the time goes in v4:
time: 59.2 us; the launch traced here: 59 us
  Pallas kernels  56.9 us (96%)
  local copies, waits for them, and re-layouts  1.48 us (2%)
  between operations  0.64 us (1%)
    pallas_call x1, Pallas kernels, per_device(): pl.pallas_call(functools.partial(kernel, sizes, n), out_shape=(jax.ShapeD...  56.9 us

profile of v4, /device:TPU:0, one launch (start us, length us, event | category | flops | bytes accessed | tf_op | source)
XLA Modules:
  0.0 59.0 jit_solution(3225851956862292445)
XLA Ops:
  0.6 56.9 %covariance.1 = (f32[32,8,1024]{2,1,0:T(8,128)S(1)}, f32[8,128]{1,0:T(8,128)S(1)}) custom-call(f32[80,8,1024]{2,1,0:T(8,128)} %pert_hbm.1, f32[32,8,1024]{2,1,0:T(8,128)} %grad_hbm.1, f32[20,1024]{1,0:T(8,128)} %hor_hbm.1, f32[1,1024]{1,0:T(1,128)} %bitcast.4, f32[8,20]{1,0:T(8,128)} %bitcast.5), custom_call_target="tpu_custom_call" | custom-call | tf_op jit(solution)/shard_map/covariance/pallas_call | solution.py:701
  57.6 0.5 slice_bitcast_fusion
  58.1 1.0 %copy.8 = f32[32,8,1024]{2,1,0:T(8,128)} copy(f32[32,8,1024]{2,1,0:T(8,128)S(1)} %get-tuple-element.8) | data formatting | bytes 2097152

commit v5 on v3

--- a/solution.py
+++ b/solution.py
@@ -11,7 +11,7 @@
 NT = (((1,), (1,)), ((), ()))
 TN = (((0,), (0,)), ((), ()))
 NN = (((1,), (0,)), ((), ()))
-UNROLL = 2
+UNROLL = 8
 BLOCKS = 4
 
 
@@ -27,18 +27,42 @@
     )
 
 
-def timetable(*stages):
-    starts = (3.5, 8.3, 12.8, 17.0, 22.9, 29.1, 32.5, 40.7)
-    paces = (2.05, 2.4, 2.7, 2.6, 2.9, 2.9, 3.0, 2.3)
-    return zip(stages, starts, paces)
+PLAN = (
+    0, 800, 100, 101, 3, 107, 106, 900, 1, 103, 201, 102, 2, 200,
+    206, 207, 104, 105, 301, 4, 203, 300, 202, 108, 1000, 307, 306, 109,
+    1300, 401, 204, 205, 302, 1100, 303, 400, 208, 407, 501, 304, 305, 406,
+    209, 402, 500, 308, 507, 309, 1200, 404, 405, 506, 403, 502, 607, 600,
+    408, 409, 601, 606, 1400, 504, 1501, 505, 503, 602, 508, 1001, 605, 509,
+    604, 603, 703, 608, 1101, 1201, 609, 700, 702, 701, 704, 1600, 1701,
+)
+
+
+def order(chunks, stages):
+    if chunks == 5:
+        entries = [(entry // 100, entry % 100) for entry in PLAN]
+    else:
+        starts = (0, 5, 10, 16, 22, 28, 34, 40)
+        timed = [(start + 2.8 * j, k, j) for k, start in enumerate(starts) if k in (0, 7) for j in range(chunks)]
+        timed += [
+            (start + 1.4 * i, k, i)
+            for k, start in enumerate(starts) if k not in (0, 7) for i in range(2 * chunks)
+        ]
+        late = 22 + 2.8 * chunks
+        timed += [
+            (4.9, 8, 0), (4.95, 9, 0), (12, 10, 0), (16, 11, 0), (18, 12, 0), (21, 13, 0),
+            (late, 14, 0), (late + 1, 15, 1), (late + 4, 10, 1), (late + 7, 11, 1),
+            (late + 9, 12, 1), (1e6, 16, 0), (2e6, 17, 1),
+        ]
+        entries = [entry[1:] for entry in sorted(timed)]
+    return [(stages[k], i) for k, i in entries]
 
 
 def kernel(
     sizes, n, pert_hbm, grad_hbm, hor_hbm, area_hbm, vert_hbm, out_ref, bg_ref,
     pert_ref, grad_ref, hor_ref, area_ref, vert_ref,
-    halves, weighted, acc, terms, first_a, first_b, second, third, raised, lifted,
+    halves, weighted, acc, terms, first, second, third, raised, lifted,
     totals, verticals, sums, weights, scaled,
-    load_p, load_s, send_h, recv_h, send_g, recv_g, send_l, recv_l, send_m, recv_m,
+    load_p, load_s, send_h, recv_h, send_g, recv_g, send_l, recv_l,
     send_t, recv_t, send_v, recv_v,
 ):
     members, levels, vectors, modes, columns = sizes
@@ -108,63 +132,65 @@
             device_id=device, device_id_type=mesh_id,
         )
 
-    def halfway(j):
+    def piece(i):
+        j, side = i // 2, i % 2
         count = (tiles + 1 - j % 2) // 2 * levels
-        return pl.ds(0, count), pl.ds(count, rows - count), count, rows - count
-
-    def half_copy(j, i, src, dst, device):
-        return remote(src, dst, send_h.at[j, i], recv_h.at[j, i], device)
-
-    def one(j):
-        a, b, na, nb = halfway(j)
-        return (
-            half_copy(j, 0, terms.at[j, :, :, not_x, a], first_a.at[j, :, :, pl.ds(0, na)], x_peer),
-            half_copy(j, 1, terms.at[j, :, not_y, :, b], first_b.at[j, :, :, pl.ds(0, nb)], y_peer),
-        )
-
-    def two(j):
-        a, b, na, nb = halfway(j)
-        return (
-            half_copy(j, 2, first_a.at[j, :, not_y, pl.ds(0, na)], second.at[j, :, a], y_peer),
-            half_copy(j, 3, first_b.at[j, :, not_x, pl.ds(0, nb)], second.at[j, :, b], x_peer),
-        )
-
-    def keeper(j):
-        return j % 2
-
-    def outer_copy(j, p, source):
+        start, size = (0, count) if side == 0 else (count, rows - count)
+        return j, side, pl.ds(start, size), size
+
+    def half_copy(i, k, src, dst, device):
+        return remote(src, dst, send_h.at[i, k], recv_h.at[i, k], device)
+
+    def one(i):
+        j, side, span, size = piece(i)
+        target = first.at[i, :, :, pl.ds(0, size)]
+        if side == 0:
+            return half_copy(i, 0, terms.at[j, :, :, not_x, span], target, x_peer)
+        return half_copy(i, 0, terms.at[j, :, not_y, :, span], target, y_peer)
+
+    def two(i):
+        j, side, span, size = piece(i)
+        index, device = (not_y, y_peer) if side == 0 else (not_x, x_peer)
+        source = first.at[i, :, index, pl.ds(0, size)]
+        return half_copy(i, 1, source, second.at[j, :, span], device)
+
+    def keeper(i):
+        return i % 2
+
+    def outer_copy(i, p, source):
+        j, side, span, size = piece(i)
         return remote(
-            second.at[j, lax.rem(h + p, outer)], third.at[j, source, p],
-            send_g.at[j, p], recv_g.at[j, source, p], (along(p), keeper(j)),
-        )
-
-    def lifted_copy(j, p, slot):
-        block = lifted.at[j, slot, y, x]
-        return remote(block, block, send_l.at[j, p], recv_l.at[j, p], (along(p), lev))
-
-    def raised_copy(j, p, slot):
+            second.at[j, lax.rem(h + p, outer), span], third.at[j, source, p, span],
+            send_g.at[i, p], recv_g.at[i, source, p], (along(p), keeper(i)),
+        )
+
+    def lifted_copy(i, p, slot):
+        j, side, span, size = piece(i)
+        block = lifted.at[j, slot, y, x, span]
+        return remote(block, block, send_l.at[i, p], recv_l.at[i, p], (along(p), lev))
+
+    def raised_copy(i, p, slot):
+        j, side, span, size = piece(i)
         return remote(
-            raised.at[j], lifted.at[j, slot, y, x],
-            send_m.at[j, p], recv_m.at[j, p], (along(p), other),
-        )
-
-    def three(j, yy, xx):
-        a, b, _, _ = halfway(j)
-        block_a = lifted.at[j, :, yy, x, a]
-        block_b = lifted.at[j, :, y, xx, b]
-        return (
-            half_copy(j, 4, block_a, block_a, y_peer),
-            half_copy(j, 5, block_b, block_b, x_peer),
-        )
-
-    def four(j, yy, xx):
-        a, b, _, _ = halfway(j)
-        block_a = lifted.at[j, :, :, xx, a]
-        block_b = lifted.at[j, :, yy, :, b]
-        return (
-            half_copy(j, 6, block_a, block_a, x_peer),
-            half_copy(j, 7, block_b, block_b, y_peer),
-        )
+            raised.at[j, span], lifted.at[j, slot, y, x, span],
+            send_g.at[i, p], recv_l.at[i, p], (along(p), other),
+        )
+
+    def three(i, yy, xx):
+        j, side, span, size = piece(i)
+        if side == 0:
+            block = lifted.at[j, :, yy, x, span]
+            return half_copy(i, 2, block, block, y_peer)
+        block = lifted.at[j, :, y, xx, span]
+        return half_copy(i, 2, block, block, x_peer)
+
+    def four(i, yy, xx):
+        j, side, span, size = piece(i)
+        if side == 0:
+            block = lifted.at[j, :, :, xx, span]
+            return half_copy(i, 3, block, block, x_peer)
+        block = lifted.at[j, :, yy, :, span]
+        return half_copy(i, 3, block, block, y_peer)
 
     def vert_copy(slot):
         block = verticals.at[slot]
@@ -280,125 +306,119 @@
 
         over_levels(step)
 
-    def send_one(j):
-        for copy in one(j):
-            copy.start()
-
-    def send_two(j):
-        a, b, na, nb = halfway(j)
-        one_a, one_b = one(j)
-        two_a, two_b = two(j)
-
-        def add_a(i, carry):
-            first_a[j, i, not_y, :na] += terms[j, i, not_y, x, a]
+    def send_one(i):
+        one(i).start()
+
+    def send_two(i):
+        j, side, span, size = piece(i)
+        one(i).wait_recv()
+
+        def add(q, carry):
+            if side == 0:
+                first[i, q, not_y, :size] += terms[j, q, not_y, x, span]
+            else:
+                first[i, q, not_x, :size] += terms[j, q, y, not_x, span]
             return carry
 
-        def add_b(i, carry):
-            first_b[j, i, not_x, :nb] += terms[j, i, y, not_x, b]
+        lax.fori_loop(0, outer, add, 0)
+        two(i).start()
+
+    def send_three(i):
+        j, side, span, size = piece(i)
+        two(i).wait_recv()
+
+        def add_second(there):
+            mine = first[i, there, y if side == 0 else x, :size]
+            second[j, there, span] += terms[j, there, y, x, span] + mine
+
+        def send_outer(p, carry):
+            add_second(lax.rem(h + p, outer))
+            outer_copy(i, p, lev).start()
             return carry
 
-        one_a.wait_recv()
-        lax.fori_loop(0, outer, add_a, 0)
-        two_a.start()
-        one_b.wait_recv()
-        lax.fori_loop(0, outer, add_b, 0)
-        two_b.start()
-
-    def add_second(j, there):
-        a, b, na, nb = halfway(j)
-        second[j, there, a] += terms[j, there, y, x, a] + first_a[j, there, y, :na]
-        second[j, there, b] += terms[j, there, y, x, b] + first_b[j, there, x, :nb]
-
-    def send_three(j):
-        for copy in two(j):
-            copy.wait_recv()
-
-        def send_outer(p, carry):
-            add_second(j, lax.rem(h + p, outer))
-            outer_copy(j, p, lev).start()
-            return carry
-
         lax.fori_loop(1, outer, send_outer, 0)
-        add_second(j, h)
-
-        @pl.when(lev != keeper(j))
+        add_second(h)
+
+        @pl.when(lev != keeper(i))
         def _():
-            outer_copy(j, 0, lev).start()
-
-    def mix(j):
-        @pl.when(lev == keeper(j))
+            outer_copy(i, 0, lev).start()
+
+    def mix(i):
+        j, side, span, size = piece(i)
+
+        @pl.when(lev == keeper(i))
         def _():
             def take(p, carry):
-                outer_copy(j, p, lev).wait_recv()
-                second[j, h] += third[j, lev, p]
-                outer_copy(j, p, other).wait_recv()
-                third[j, other, 0] += third[j, other, p]
+                outer_copy(i, p, lev).wait_send()
+                outer_copy(i, p, lev).wait_recv()
+                second[j, h, span] += third[j, lev, p, span]
+                outer_copy(i, p, other).wait_recv()
+                third[j, other, 0, span] += third[j, other, p, span]
                 return carry
 
-            outer_copy(j, 0, other).wait_recv()
+            outer_copy(i, 0, other).wait_recv()
             lax.fori_loop(1, outer, take, 0)
 
             def wide(block):
                 return jnp.concatenate(
-                    [block[i * levels : (i + 1) * levels] for i in range(tiles)], axis=1
+                    [block[t : t + levels] for t in range(0, size, levels)], axis=1
                 )
 
             far = verticals[other][:, :vmodes]
-            control = exact_dot(vert_ref[...], wide(second[j, h]), TN) + exact_dot(
-                far, wide(third[j, other, 0]), TN
+            control = exact_dot(vert_ref[...], wide(second[j, h, span]), TN) + exact_dot(
+                far, wide(third[j, other, 0, span]), TN
             )
             near_lifted = exact_dot(vert_ref[...], control, NN)
             far_lifted = exact_dot(far, control, NN)
             square = jnp.zeros((1, LANES), jnp.float32)
-            for i in range(tiles):
-                lanes = slice(i * LANES, (i + 1) * LANES)
-                part = slice(i * levels, (i + 1) * levels)
+            for t in range(size // levels):
+                lanes = slice(t * LANES, (t + 1) * LANES)
+                part = pl.ds(span.start + t * levels, levels)
                 lifted[j, h, y, x, part, :] = near_lifted[:, lanes]
                 raised[j, part, :] = far_lifted[:, lanes]
                 square = square + jnp.sum(
                     control[:, lanes] * control[:, lanes], axis=0, keepdims=True
                 )
-            sums[j : j + 1, :] = square
+            sums[j : j + 1, :] = sums[j : j + 1, :] + square
 
             def start_lifted(p, carry):
-                lifted_copy(j, p, h).start()
-                raised_copy(j, p, h).start()
+                lifted_copy(i, p, h).start()
+                raised_copy(i, p, h).start()
                 return carry
 
-            raised_copy(j, 0, h).start()
+            raised_copy(i, 0, h).start()
             lax.fori_loop(1, outer, start_lifted, 0)
 
-    def send_g2(j):
-        @pl.when(lev == keeper(j))
+    def send_g2(i):
+        @pl.when(lev == keeper(i))
         def _():
             def take(p, carry):
-                lifted_copy(j, p, lax.rem(h + outer - p, outer)).wait_recv()
+                lifted_copy(i, p, lax.rem(h + outer - p, outer)).wait_recv()
                 return carry
 
             lax.fori_loop(1, outer, take, 0)
 
-        @pl.when(lev != keeper(j))
+        @pl.when(lev != keeper(i))
         def _():
             def take(p, carry):
-                raised_copy(j, p, lax.rem(h + outer - p, outer)).wait_recv()
+                raised_copy(i, p, lax.rem(h + outer - p, outer)).wait_recv()
                 return carry
 
             lax.fori_loop(0, outer, take, 0)
 
-        for copy in three(j, y, x):
-            copy.start()
-
-    def send_g3(j):
-        three_a, three_b = three(j, not_y, not_x)
-        four_a, four_b = four(j, y, x)
-        three_a.wait_recv()
-        four_a.start()
-        three_b.wait_recv()
-        four_b.start()
+        three(i, y, x).start()
+
+    def send_g3(i):
+        three(i, not_y, not_x).wait_recv()
+        four(i, y, x).start()
+
+    started = []
 
     def forward(j):
-        for copy in four(j, not_y, not_x):
-            copy.wait_recv()
+        fresh = not started
+        started.append(j)
+        for i in (2 * j, 2 * j + 1):
+            four(i, not_y, not_x).wait_recv()
         flat = lifted.at[j].reshape(n * rows, LANES)
         width = 256
 
@@ -409,7 +429,7 @@
                 cols = slice(c, c + width)
                 rhs = jnp.concatenate([halves[l, :, cols], halves[l, :members, cols]], axis=0)
                 spread = lax.dot_general(lhs, rhs, TN, preferred_element_type=jnp.float32)
-                value = None if j == 0 else acc[l, :, cols]
+                value = None if fresh else acc[l, :, cols]
                 for g in range(group):
                     b = j * group + g
                     term = spread[g * vectors : (g + 1) * vectors] * scaled[b : b + 1, cols]
@@ -467,47 +487,34 @@
             for v in range(0, vectors, 8):
                 out_ref[v : v + 8, :, lanes] = jnp.swapaxes(acc[:, v : v + 8, lanes], 0, 1)
 
-    plan = [
-        (start + pace * j, stage, j)
-        for stage, start, pace in timetable(
-            adjoint, send_one, send_two, send_three, mix, send_g2, send_g3, forward
-        )
-        for j in range(chunks)
-    ]
-    last = chunks - 5
-    plan += [
-        (8.2, meet, 0), (8.65, set_stats, 0), (13.0, send_total_y, 0), (16.7, send_total_c, 0),
-        (19.0, send_total_outer, 0), (20.0, take_vert, 0), (26.0, take_stats, 0),
-        (36.0 + 3 * last, gather_sums, 1), (38.85 + 3 * last, send_total_y, 1),
-        (41.5 + 3 * last, send_total_c, 1), (43.5 + 3 * last, send_total_outer, 1),
-        (1000.0, finish_out, 0), (1001.0, finish_sums, 1),
-    ]
     prepare()
-    for _, stage, j in sorted(plan, key=lambda entry: entry[0]):
-        stage(j)
-
-    for j in range(chunks):
-        for copy in one(j) + two(j) + three(j, y, x) + four(j, y, x):
+    for stage, i in order(chunks, (
+        adjoint, send_one, send_two, send_three, mix, send_g2, send_g3, forward, meet, set_stats,
+        send_total_y, send_total_c, send_total_outer, take_vert, take_stats, gather_sums,
+        finish_out, finish_sums,
+    )):
+        stage(i)
+
+    for i in range(2 * chunks):
+        for copy in (one(i), two(i), three(i, y, x), four(i, y, x)):
             copy.wait_send()
 
-        def sent_outer(p, carry):
-            outer_copy(j, p, lev).wait_send()
-            return carry
-
-        lax.fori_loop(1, outer, sent_outer, 0)
-
-        @pl.when(lev != keeper(j))
-        def _():
-            outer_copy(j, 0, lev).wait_send()
-
-        @pl.when(lev == keeper(j))
+        @pl.when(lev != keeper(i))
         def _():
             def sent(p, carry):
-                lifted_copy(j, p, h).wait_send()
-                raised_copy(j, p, h).wait_send()
+                outer_copy(i, p, lev).wait_send()
                 return carry
 
-            raised_copy(j, 0, h).wait_send()
+            lax.fori_loop(0, outer, sent, 0)
+
+        @pl.when(lev == keeper(i))
+        def _():
+            def sent(p, carry):
+                lifted_copy(i, p, h).wait_send()
+                raised_copy(i, p, h).wait_send()
+                return carry
+
+            raised_copy(i, 0, h).wait_send()
             lax.fori_loop(1, outer, sent, 0)
 
     for k in range(2):
@@ -557,8 +564,7 @@
             pltpu.VMEM((levels, vectors, columns), f32),
             pltpu.VMEM((levels, vectors, columns), f32),
             pltpu.VMEM((chunks, outer, 2, 2, rows, LANES), f32),
-            pltpu.VMEM((chunks, outer, 2, most, LANES), f32),
-            pltpu.VMEM((chunks, outer, 2, most, LANES), f32),
+            pltpu.VMEM((2 * chunks, outer, 2, most, LANES), f32),
             pltpu.VMEM((chunks, outer, rows, LANES), f32),
             pltpu.VMEM((chunks, 2, outer, rows, LANES), f32),
             pltpu.VMEM((chunks, rows, LANES), f32),
@@ -569,10 +575,9 @@
             pltpu.VMEM((8, LANES), f32),
             pltpu.VMEM((modes, columns), f32),
             dma((2, BLOCKS)), dma((3,)),
-            dma((chunks, 8)), dma((chunks, 8)),
-            dma((chunks, outer)), dma((chunks, 2, outer)),
-            dma((chunks, outer)), dma((chunks, outer)),
-            dma((chunks, outer)), dma((chunks, outer)),
+            dma((2 * chunks, 4)), dma((2 * chunks, 4)),
+            dma((2 * chunks, outer)), dma((2 * chunks, 2, outer)),
+            dma((2 * chunks, outer)), dma((2 * chunks, outer)),
             dma((2, 6 + outer)), dma((2, 6 + outer)),
             dma((1,)), dma((1,)),
         ],

time: 58.5 us -> 51.4 us (0.88)
  Pallas kernels: 56.2 us -> 49.2 us
    pallas_call x1, Pallas kernels: 56.2 us -> 49.2 us  [per_device(): pl.pallas_call(functools.partial(kernel, sizes, n), out_shape=(jax.ShapeD...]
where the time goes in v5:
time: 51.4 us; the launch traced here: 51.3 us
  Pallas kernels  49.2 us (96%)
  local copies, waits for them, and re-layouts  1.48 us (3%)
  between operations  0.64 us (1%)
    pallas_call x1, Pallas kernels, per_device(): pl.pallas_call(functools.partial(kernel, sizes, n), out_shape=(jax.ShapeD...  49.2 us

profile of v5, /device:TPU:0, one launch (start us, length us, event | category | flops | bytes accessed | tf_op | source)
XLA Modules:
  0.0 51.3 jit_solution(18233237292737841665)
XLA Ops:
  0.6 49.2 %covariance.1 = (f32[32,8,1024]{2,1,0:T(8,128)S(1)}, f32[8,128]{1,0:T(8,128)S(1)}) custom-call(f32[80,8,1024]{2,1,0:T(8,128)} %pert_hbm.1, f32[32,8,1024]{2,1,0:T(8,128)} %grad_hbm.1, f32[20,1024]{1,0:T(8,128)} %hor_hbm.1, f32[1,1024]{1,0:T(1,128)} %bitcast.4, f32[8,20]{1,0:T(8,128)} %bitcast.5), custom_call_target="tpu_custom_call" | custom-call | tf_op jit(solution)/shard_map/covariance/pallas_call | solution.py:549
  49.8 0.5 %slice_bitcast_fusion = f32[32]{0:T(128)} fusion(f32[8,128]{1,0:T(8,128)S(1)} %get-tuple-element.5), kind=kLoop, calls=%fused_computation | loop fusion | bytes 256 | tf_op jit(solution)/shard_map/squeeze | solution.py:592
  50.3 1.0 %copy.8 = f32[32,8,1024]{2,1,0:T(8,128)} copy(f32[32,8,1024]{2,1,0:T(8,128)S(1)} %get-tuple-element.8) | data formatting | bytes 2097152

commit v6 on v5

--- a/solution.py
+++ b/solution.py
@@ -13,6 +13,7 @@
 NN = (((1,), (0,)), ((), ()))
 UNROLL = 8
 BLOCKS = 4
+Z_FIRST = (0, 3)
 
 
 def split(x):
@@ -28,12 +29,13 @@
 
 
 PLAN = (
-    0, 800, 100, 101, 3, 107, 106, 900, 1, 103, 201, 102, 2, 200,
-    206, 207, 104, 105, 301, 4, 203, 300, 202, 108, 1000, 307, 306, 109,
-    1300, 401, 204, 205, 302, 1100, 303, 400, 208, 407, 501, 304, 305, 406,
-    209, 402, 500, 308, 507, 309, 1200, 404, 405, 506, 403, 502, 607, 600,
-    408, 409, 601, 606, 1400, 504, 1501, 505, 503, 602, 508, 1001, 605, 509,
-    604, 603, 703, 608, 1101, 1201, 609, 700, 702, 701, 704, 1600, 1701,
+    1, 800, 102, 103, 3, 107, 106, 2, 105, 104, 0, 100, 202, 101,
+    900, 206, 207, 4, 108, 1000, 204, 302, 203, 109, 205, 307, 201, 306,
+    1100, 304, 303, 208, 1200, 200, 305, 209, 301, 1300, 402, 407, 1803, 300,
+    308, 403, 309, 406, 503, 404, 1800, 401, 502, 400, 405, 603, 1400, 500,
+    507, 408, 409, 602, 506, 504, 1903, 1501, 600, 501, 607, 505, 606, 508,
+    1001, 509, 604, 601, 1900, 605, 608, 609, 703, 1101, 1201, 701, 702, 704,
+    700, 1600, 1701,
 )
 
 
@@ -47,6 +49,7 @@
             (start + 1.4 * i, k, i)
             for k, start in enumerate(starts) if k not in (0, 7) for i in range(2 * chunks)
         ]
+        timed += [(start + 1.4 * i, k, i) for k, start in ((18, 19), (19, 37)) for i in Z_FIRST]
         late = 22 + 2.8 * chunks
         timed += [
             (4.9, 8, 0), (4.95, 9, 0), (12, 10, 0), (16, 11, 0), (18, 12, 0), (21, 13, 0),
@@ -61,7 +64,7 @@
     sizes, n, pert_hbm, grad_hbm, hor_hbm, area_hbm, vert_hbm, out_ref, bg_ref,
     pert_ref, grad_ref, hor_ref, area_ref, vert_ref,
     halves, weighted, acc, terms, first, second, third, raised, lifted,
-    totals, verticals, sums, weights, scaled,
+    z_in, z_sum, plane, totals, verticals, sums, weights, scaled,
     load_p, load_s, send_h, recv_h, send_g, recv_g, send_l, recv_l,
     send_t, recv_t, send_v, recv_v,
 ):
@@ -157,6 +160,57 @@
     def keeper(i):
         return i % 2
 
+    def z_copy(i, p):
+        j, side, span, size = piece(i)
+        return remote(
+            terms.at[j, lax.rem(h + p, outer), :, :, span],
+            z_in.at[Z_FIRST.index(i), p, :, :, pl.ds(0, size)],
+            send_g.at[i, p], recv_g.at[i, lev, p], (along(p), lev),
+        )
+
+    def plane_one(i):
+        j, side, span, size = piece(i)
+        k = Z_FIRST.index(i)
+        source = z_sum.at[k, :, not_x] if side == 0 else z_sum.at[k, not_y]
+        rows_ = pl.ds(0, size)
+        source = source.at[:, rows_]
+        target = plane.at[k, :, rows_]
+        return half_copy(i, 0, source, target, x_peer if side == 0 else y_peer)
+
+    def plane_two(i):
+        j, side, span, size = piece(i)
+        index, device = (not_y, y_peer) if side == 0 else (not_x, x_peer)
+        source = plane.at[Z_FIRST.index(i), index, pl.ds(0, size)]
+        return half_copy(i, 1, source, second.at[j, h, span], device)
+
+    def back_one(i, yy, xx):
+        j, side, span, size = piece(i)
+        if side == 0:
+            block = lifted.at[j, h, yy, x, span]
+            return half_copy(i, 2, block, block, y_peer)
+        block = lifted.at[j, h, y, xx, span]
+        return half_copy(i, 2, block, block, x_peer)
+
+    def back_two(i, yy, xx):
+        j, side, span, size = piece(i)
+        if side == 0:
+            block = lifted.at[j, h, :, xx, span]
+            return half_copy(i, 3, block, block, x_peer)
+        block = lifted.at[j, h, yy, :, span]
+        return half_copy(i, 3, block, block, y_peer)
+
+    def back_z(i, p, slot):
+        j, side, span, size = piece(i)
+        block = lifted.at[j, slot, :, :, span]
+        return remote(block, block, send_l.at[i, p], recv_l.at[i, p], (along(p), lev))
+
+    def each_outer(step):
+        def body(p, carry):
+            step(p)
+            return carry
+
+        lax.fori_loop(1, outer, body, 0)
+
     def outer_copy(i, p, source):
         j, side, span, size = piece(i)
         return remote(
@@ -307,10 +361,24 @@
         over_levels(step)
 
     def send_one(i):
-        one(i).start()
+        if i in Z_FIRST:
+            each_outer(lambda p: z_copy(i, p).start())
+        else:
+            one(i).start()
 
     def send_two(i):
         j, side, span, size = piece(i)
+        if i in Z_FIRST:
+            k = Z_FIRST.index(i)
+            z_sum[k, :, :, :size] = terms[j, h, :, :, span]
+
+            def take(p):
+                z_copy(i, p).wait_recv()
+                z_sum[k, :, :, :size] += z_in[k, p, :, :, :size]
+
+            each_outer(take)
+            plane_one(i).start()
+            return
         one(i).wait_recv()
 
         def add(q, carry):
@@ -325,6 +393,15 @@
 
     def send_three(i):
         j, side, span, size = piece(i)
+        if i in Z_FIRST:
+            k = Z_FIRST.index(i)
+            plane_one(i).wait_recv()
+            if side == 0:
+                plane[k, not_y, :size] += z_sum[k, not_y, x, :size]
+            else:
+                plane[k, not_x, :size] += z_sum[k, y, not_x, :size]
+            plane_two(i).start()
+            return
         two(i).wait_recv()
 
         def add_second(there):
@@ -338,6 +415,16 @@
 
         lax.fori_loop(1, outer, send_outer, 0)
         add_second(h)
+
+        @pl.when(lev != keeper(i))
+        def _():
+            outer_copy(i, 0, lev).start()
+
+    def z_own(i):
+        j, side, span, size = piece(i)
+        k = Z_FIRST.index(i)
+        plane_two(i).wait_recv()
+        second[j, h, span] += z_sum[k, y, x, :size] + plane[k, y if side == 0 else x, :size]
 
         @pl.when(lev != keeper(i))
         def _():
@@ -357,7 +444,8 @@
                 return carry
 
             outer_copy(i, 0, other).wait_recv()
-            lax.fori_loop(1, outer, take, 0)
+            if i not in Z_FIRST:
+                lax.fori_loop(1, outer, take, 0)
 
             def wide(block):
                 return jnp.concatenate(
@@ -387,9 +475,18 @@
                 return carry
 
             raised_copy(i, 0, h).start()
-            lax.fori_loop(1, outer, start_lifted, 0)
+            if i not in Z_FIRST:
+                lax.fori_loop(1, outer, start_lifted, 0)
 
     def send_g2(i):
+        if i in Z_FIRST:
+            @pl.when(lev != keeper(i))
+            def _():
+                raised_copy(i, 0, h).wait_recv()
+
+            back_one(i, y, x).start()
+            return
+
         @pl.when(lev == keeper(i))
         def _():
             def take(p, carry):
@@ -409,8 +506,16 @@
         three(i, y, x).start()
 
     def send_g3(i):
-        three(i, not_y, not_x).wait_recv()
-        four(i, y, x).start()
+        if i in Z_FIRST:
+            back_one(i, not_y, not_x).wait_recv()
+            back_two(i, y, x).start()
+        else:
+            three(i, not_y, not_x).wait_recv()
+            four(i, y, x).start()
+
+    def send_g4(i):
+        back_two(i, not_y, not_x).wait_recv()
+        each_outer(lambda p: back_z(i, p, h).start())
 
     started = []
 
@@ -418,7 +523,10 @@
         fresh = not started
         started.append(j)
         for i in (2 * j, 2 * j + 1):
-            four(i, not_y, not_x).wait_recv()
+            if i in Z_FIRST:
+                each_outer(lambda p: back_z(i, p, lax.rem(h + outer - p, outer)).wait_recv())
+            else:
+                four(i, not_y, not_x).wait_recv()
         flat = lifted.at[j].reshape(n * rows, LANES)
         width = 256
 
@@ -491,11 +599,26 @@
     for stage, i in order(chunks, (
         adjoint, send_one, send_two, send_three, mix, send_g2, send_g3, forward, meet, set_stats,
         send_total_y, send_total_c, send_total_outer, take_vert, take_stats, gather_sums,
-        finish_out, finish_sums,
+        finish_out, finish_sums, z_own, send_g4,
     )):
         stage(i)
 
     for i in range(2 * chunks):
+        if i in Z_FIRST:
+            for copy in (plane_one(i), plane_two(i), back_one(i, y, x), back_two(i, y, x)):
+                copy.wait_send()
+            each_outer(lambda p: z_copy(i, p).wait_send())
+            each_outer(lambda p: back_z(i, p, h).wait_send())
+
+            @pl.when(lev != keeper(i))
+            def _():
+                outer_copy(i, 0, lev).wait_send()
+
+            @pl.when(lev == keeper(i))
+            def _():
+                raised_copy(i, 0, h).wait_send()
+
+            continue
         for copy in (one(i), two(i), three(i, y, x), four(i, y, x)):
             copy.wait_send()
 
@@ -569,6 +692,9 @@
             pltpu.VMEM((chunks, 2, outer, rows, LANES), f32),
             pltpu.VMEM((chunks, rows, LANES), f32),
             pltpu.VMEM((chunks, outer, 2, 2, rows, LANES), f32),
+            pltpu.VMEM((len(Z_FIRST), outer, 2, 2, most, LANES), f32),
+            pltpu.VMEM((len(Z_FIRST), 2, 2, most, LANES), f32),
+            pltpu.VMEM((len(Z_FIRST), 2, most, LANES), f32),
             pltpu.VMEM((2, 6 + outer, 8, LANES), f32),
             pltpu.VMEM((2, levels, LANES), f32),
             pltpu.VMEM((8, LANES), f32),

time: 51.4 us -> 48.5 us (0.944)
  Pallas kernels: 49.2 us -> 46.3 us
    pallas_call x1, Pallas kernels: 49.2 us -> 46.3 us  [per_device(): pl.pallas_call(functools.partial(kernel, sizes, n), out_shape=(jax.ShapeD...]
where the time goes in v6:
time: 48.5 us; the launch traced here: 48.4 us
  Pallas kernels  46.3 us (95%)
  local copies, waits for them, and re-layouts  1.48 us (3%)
  between operations  0.64 us (1%)
    pallas_call x1, Pallas kernels, per_device(): pl.pallas_call(functools.partial(kernel, sizes, n), out_shape=(jax.ShapeD...  46.3 us

profile of v6, /device:TPU:0, one launch (start us, length us, event | category | flops | bytes accessed | tf_op | source)
XLA Modules:
  0.0 48.4 jit_solution(13639216503513814708)
XLA Ops:
  0.6 46.3 %covariance.1 = (f32[32,8,1024]{2,1,0:T(8,128)S(1)}, f32[8,128]{1,0:T(8,128)S(1)}) custom-call(f32[80,8,1024]{2,1,0:T(8,128)} %pert_hbm.1, f32[32,8,1024]{2,1,0:T(8,128)} %grad_hbm.1, f32[20,1024]{1,0:T(8,128)} %hor_hbm.1, f32[1,1024]{1,0:T(1,128)} %bitcast.4, f32[8,20]{1,0:T(8,128)} %bitcast.5), custom_call_target="tpu_custom_call" | custom-call | tf_op jit(solution)/shard_map/covariance/pallas_call | solution.py:672
  46.9 0.5 %slice_bitcast_fusion = f32[32]{0:T(128)} fusion(f32[8,128]{1,0:T(8,128)S(1)} %get-tuple-element.5), kind=kLoop, calls=%fused_computation | loop fusion | bytes 256 | tf_op jit(solution)/shard_map/squeeze | solution.py:718
  47.4 1.0 %copy.8 = f32[32,8,1024]{2,1,0:T(8,128)} copy(f32[32,8,1024]{2,1,0:T(8,128)S(1)} %get-tuple-element.8) | data formatting | bytes 2097152

commit v7 on v6

--- a/solution.py
+++ b/solution.py
@@ -12,8 +12,9 @@
 TN = (((0,), (0,)), ((), ()))
 NN = (((1,), (0,)), ((), ()))
 UNROLL = 8
-BLOCKS = 4
-Z_FIRST = (0, 3)
+BLOCKS = 2
+OUT_BLOCKS = 2
+Z_FIRST = (0, 4)
 
 
 def split(x):
@@ -29,13 +30,13 @@
 
 
 PLAN = (
-    1, 800, 102, 103, 3, 107, 106, 2, 105, 104, 0, 100, 202, 101,
-    900, 206, 207, 4, 108, 1000, 204, 302, 203, 109, 205, 307, 201, 306,
-    1100, 304, 303, 208, 1200, 200, 305, 209, 301, 1300, 402, 407, 1803, 300,
-    308, 403, 309, 406, 503, 404, 1800, 401, 502, 400, 405, 603, 1400, 500,
-    507, 408, 409, 602, 506, 504, 1903, 1501, 600, 501, 607, 505, 606, 508,
-    1001, 509, 604, 601, 1900, 605, 608, 609, 703, 1101, 1201, 701, 702, 704,
-    700, 1600, 1701,
+    0, 800, 101, 100, 3, 107, 106, 4, 109, 108, 2, 104, 201, 105,
+    1, 207, 206, 103, 209, 208, 200, 301, 900, 205, 306, 102, 307, 309,
+    300, 203, 1000, 305, 204, 308, 1300, 401, 202, 1800, 406, 400, 303, 407,
+    304, 500, 302, 408, 1100, 409, 1804, 501, 506, 404, 1200, 600, 403, 405,
+    504, 507, 402, 601, 606, 1900, 604, 509, 508, 1400, 1501, 607, 503, 502,
+    505, 608, 1904, 1001, 609, 603, 605, 602, 1101, 703, 1201, 704, 700, 701,
+    702, 1600, 1701,
 )
 
 
@@ -61,9 +62,9 @@
 
 
 def kernel(
-    sizes, n, pert_hbm, grad_hbm, hor_hbm, area_hbm, vert_hbm, out_ref, bg_ref,
+    sizes, n, pert_hbm, grad_hbm, hor_hbm, area_hbm, vert_hbm, acc, bg_ref,
     pert_ref, grad_ref, hor_ref, area_ref, vert_ref,
-    halves, weighted, acc, terms, first, second, third, raised, lifted,
+    halves, weighted, terms, first, second, third, raised, lifted,
     z_in, z_sum, plane, totals, verticals, sums, weights, scaled,
     load_p, load_s, send_h, recv_h, send_g, recv_g, send_l, recv_l,
     send_t, recv_t, send_v, recv_v,
@@ -76,6 +77,7 @@
     tiles = rows // levels
     outer = n // 4
     used = members * levels
+    apart = -(-members // LANES) * LANES
     me = lax.axis_index("col")
     lev = lax.axis_index("lev")
     other = 1 - lev
@@ -320,7 +322,7 @@
                 for k in range(0, members, 16):
                     high, low = split(jnp.swapaxes(pert_ref[k : k + 16, :, lanes], 0, 1))
                     halves[:, k : k + 16, lanes] = high
-                    halves[:, members + k : members + k + 16, lanes] = low
+                    halves[:, apart + k : apart + k + 16, lanes] = low
                 for v in range(0, vectors, 8):
                     block = jnp.swapaxes(grad_ref[v : v + 8, :, lanes], 0, 1)
                     weighted[:, v : v + 8, lanes] = block * area[:, lanes]
@@ -352,11 +354,12 @@
                 [base * hor_ref[b : b + 1, :] for b in range(j * group, (j + 1) * group)],
                 axis=0,
             )
-            both = jnp.concatenate(split(products), axis=0)
-            out = lax.dot_general(halves[l], both, NT, preferred_element_type=jnp.float32)
-            flat[pl.ds(l, members, stride=levels), :] = out[:members, :LANES] + (
-                out[members:, :LANES] + out[:members, LANES:]
+            out = lax.dot_general(
+                jnp.concatenate(split(products), axis=0), halves[l], NT,
+                preferred_element_type=jnp.float32,
             )
+            value = out[:LANES, :members] + (out[:LANES, apart:] + out[LANES:, :members])
+            flat[pl.ds(l, members, stride=levels), :] = value.T
 
         over_levels(step)
 
@@ -535,7 +538,8 @@
             lhs = jnp.concatenate([high, high, low], axis=0)
             for c in range(0, columns, width):
                 cols = slice(c, c + width)
-                rhs = jnp.concatenate([halves[l, :, cols], halves[l, :members, cols]], axis=0)
+                top = halves[l, :members, cols]
+                rhs = jnp.concatenate([top, halves[l, apart:, cols], top], axis=0)
                 spread = lax.dot_general(lhs, rhs, TN, preferred_element_type=jnp.float32)
                 value = None if fresh else acc[l, :, cols]
                 for g in range(group):
@@ -590,10 +594,7 @@
         send_total_x(k)
 
     def finish_out(k):
-        for c in range(0, columns, LANES):
-            lanes = slice(c, c + LANES)
-            for v in range(0, vectors, 8):
-                out_ref[v : v + 8, :, lanes] = jnp.swapaxes(acc[:, v : v + 8, lanes], 0, 1)
+        pass
 
     prepare()
     for stage, i in order(chunks, (
@@ -650,6 +651,15 @@
 
         lax.fori_loop(1, outer, sent_total, 0)
     vert_copy(lev).wait_send()
+
+
+def output_kernel(acc_ref, halved_ref, out_ref, bg_ref):
+    vectors, levels, width = out_ref.shape
+    bg_ref[...] = halved_ref[:1, :vectors]
+    for c in range(0, width, LANES):
+        lanes = slice(c, c + LANES)
+        for v in range(0, vectors, 8):
+            out_ref[v : v + 8, :, lanes] = jnp.swapaxes(acc_ref[:, v : v + 8, lanes], 0, 1)
 
 
 def per_device(perturbations, gradient, horizontal, area, vertical):
@@ -662,6 +672,7 @@
     tiles = max(2, -(-members // n))
     rows = tiles * levels
     outer = n // 4
+    apart = -(-members // LANES) * LANES
     most = (tiles + 1) // 2 * levels
     f32 = jnp.float32
     vmem = pl.BlockSpec(memory_space=pltpu.VMEM)
@@ -669,10 +680,10 @@
 
     held = chunks * n * rows * LANES * 4 * 9 // 2
     limit = min(60 * 2**20, held + 20 * 2**20)
-    increment, background = pl.pallas_call(
+    by_level, halved = pl.pallas_call(
         functools.partial(kernel, sizes, n),
         out_shape=(
-            jax.ShapeDtypeStruct((vectors, levels, columns), f32),
+            jax.ShapeDtypeStruct((levels, vectors, columns), f32),
             jax.ShapeDtypeStruct((8, LANES), f32),
         ),
         in_specs=[pl.BlockSpec(memory_space=pltpu.HBM)] * 5,
@@ -683,8 +694,7 @@
             pltpu.VMEM((modes, columns), f32),
             pltpu.VMEM((1, columns), f32),
             pltpu.VMEM((levels, vertical.shape[0]), f32),
-            pltpu.VMEM((levels, 2 * members, columns), jnp.bfloat16),
-            pltpu.VMEM((levels, vectors, columns), f32),
+            pltpu.VMEM((levels, apart + members, columns), jnp.bfloat16),
             pltpu.VMEM((levels, vectors, columns), f32),
             pltpu.VMEM((chunks, outer, 2, 2, rows, LANES), f32),
             pltpu.VMEM((2 * chunks, outer, 2, most, LANES), f32),
@@ -715,7 +725,26 @@
         pltpu.with_memory_space_constraint(array, pltpu.HBM)
         for array in (perturbations, gradient, horizontal, area.reshape(1, columns), vertical.T)
     ))
-    return increment, background[0, :vectors]
+    width = columns // OUT_BLOCKS
+    increment, background = pl.pallas_call(
+        output_kernel,
+        grid=(OUT_BLOCKS,),
+        out_shape=(
+            jax.ShapeDtypeStruct((vectors, levels, columns), f32),
+            jax.ShapeDtypeStruct((1, vectors), f32),
+        ),
+        in_specs=[
+            pl.BlockSpec((levels, vectors, width), lambda c: (0, 0, c)),
+            pl.BlockSpec((8, LANES), lambda c: (0, 0)),
+        ],
+        out_specs=(
+            pl.BlockSpec((vectors, levels, width), lambda c: (0, 0, c)),
+            pl.BlockSpec((1, vectors), lambda c: (0, 0)),
+        ),
+        compiler_params=pltpu.CompilerParams(vmem_limit_bytes=8 * 2**20),
+        name="output",
+    )(by_level, halved)
+    return increment, background.reshape(vectors)
 
 
 def solution(mesh):

time: 48.5 us -> 47.2 us (0.973)
  local copies, waits for them, and re-layouts: 1.48 us -> 0 us
    pallas_call x0 -> x1, Pallas kernels: none -> 1.17 us  [per_device(): pl.pallas_call(output_kernel, grid=(OUT_BLOCKS,), out_shape=(jax.ShapeDty...]
    pallas_call x1, Pallas kernels: 46.3 us -> 45.2 us  [per_device(): pl.pallas_call(functools.partial(kernel, sizes, n), out_shape=(jax.ShapeD...]
    unnamed x1 -> x0, local copies, waits for them, and re-layouts: 0.97 us -> none
    squeeze x1 -> x0, local copies, waits for them, and re-layouts: 0.51 us -> none  [per_device(): return (increment, background[0, :vectors])]
where the time goes in v7:
time: 47.2 us; the launch traced here: 47 us
  Pallas kernels  46.4 us (98%)
  between operations  0.64 us (1%)
    pallas_call x1, Pallas kernels, per_device(): pl.pallas_call(functools.partial(kernel, sizes, n), out_shape=(jax.ShapeD...  45.2 us
    pallas_call x1, Pallas kernels, per_device(): pl.pallas_call(output_kernel, grid=(OUT_BLOCKS,), out_shape=(jax.ShapeDty...  1.17 us

profile of v7, /device:TPU:0, one launch (start us, length us, event | category | flops | bytes accessed | tf_op | source)
XLA Modules:
  0.0 47.0 jit_solution(12580260990789587591)
XLA Ops:
  0.6 45.2 %covariance.1 = (f32[8,32,1024]{2,1,0:T(8,128)S(1)}, f32[8,128]{1,0:T(8,128)S(1)}) custom-call(f32[80,8,1024]{2,1,0:T(8,128)} %pert_hbm.1, f32[32,8,1024]{2,1,0:T(8,128)} %grad_hbm.1, f32[20,1024]{1,0:T(8,128)} %hor_hbm.1, f32[1,1024]{1,0:T(1,128)} %bitcast.3, f32[8,20]{1,0:T(8,128)} %bitcast.4), custom_call_target="tpu_custom_call" | custom-call | tf_op jit(solution)/shard_map/covariance/pallas_call | solution.py:683
  45.9 1.2 %output.1 = (f32[32,8,1024]{2,1,0:T(8,128)}, f32[1,32]{1,0:T(1,128)}) custom-call(f32[8,32,1024]{2,1,0:T(8,128)S(1)} %get-tuple-element.6.acc_ref, f32[8,128]{1,0:T(8,128)S(1)} %get-tuple-element.7.halved_ref), custom_call_target="tpu_custom_call" | custom-call | tf_op jit(solution)/shard_map/output/pallas_call | solution.py:729

commit v8 on v7

--- a/solution.py
+++ b/solution.py
@@ -30,13 +30,13 @@
 
 
 PLAN = (
-    0, 800, 101, 100, 3, 107, 106, 4, 109, 108, 2, 104, 201, 105,
-    1, 207, 206, 103, 209, 208, 200, 301, 900, 205, 306, 102, 307, 309,
-    300, 203, 1000, 305, 204, 308, 1300, 401, 202, 1800, 406, 400, 303, 407,
-    304, 500, 302, 408, 1100, 409, 1804, 501, 506, 404, 1200, 600, 403, 405,
-    504, 507, 402, 601, 606, 1900, 604, 509, 508, 1400, 1501, 607, 503, 502,
-    505, 608, 1904, 1001, 609, 603, 605, 602, 1101, 703, 1201, 704, 700, 701,
-    702, 1600, 1701,
+    2, 800, 104, 105, 3, 106, 107, 4, 108, 109, 0, 100, 205, 1,
+    103, 207, 209, 208, 204, 206, 101, 305, 900, 102, 307, 203, 309, 304,
+    308, 306, 200, 202, 1000, 1300, 405, 201, 303, 1804, 407, 404, 300, 302,
+    1100, 504, 301, 408, 505, 1200, 409, 1800, 403, 604, 400, 507, 406, 500,
+    605, 402, 401, 508, 1400, 1904, 607, 1501, 600, 509, 503, 506, 608, 502,
+    1900, 1001, 501, 609, 603, 606, 1101, 602, 1201, 601, 702, 704, 703, 701,
+    700, 1600, 1701,
 )
 
 

time: 47.2 us -> 46.9 us (level)
  no operation moved by 1% of the time
where the time goes in v8:
time: 46.9 us; the launch traced here: 46.8 us
  Pallas kernels  46.1 us (98%)
  between operations  0.64 us (1%)
    pallas_call x1, Pallas kernels, per_device(): pl.pallas_call(functools.partial(kernel, sizes, n), out_shape=(jax.ShapeD...  44.9 us
    pallas_call x1, Pallas kernels, per_device(): pl.pallas_call(output_kernel, grid=(OUT_BLOCKS,), out_shape=(jax.ShapeDty...  1.17 us

profile of v8, /device:TPU:0, one launch (start us, length us, event | category | flops | bytes accessed | tf_op | source)
XLA Modules:
  0.0 46.8 jit_solution(6861595997520361519)
XLA Ops:
  0.6 44.9 %covariance.1 = (f32[8,32,1024]{2,1,0:T(8,128)S(1)}, f32[8,128]{1,0:T(8,128)S(1)}) custom-call(f32[80,8,1024]{2,1,0:T(8,128)} %pert_hbm.1, f32[32,8,1024]{2,1,0:T(8,128)} %grad_hbm.1, f32[20,1024]{1,0:T(8,128)} %hor_hbm.1, f32[1,1024]{1,0:T(1,128)} %bitcast.3, f32[8,20]{1,0:T(8,128)} %bitcast.4), custom_call_target="tpu_custom_call" | custom-call | tf_op jit(solution)/shard_map/covariance/pallas_call | solution.py:683
  45.6 1.2 %output.1 = (f32[32,8,1024]{2,1,0:T(8,128)}, f32[1,32]{1,0:T(1,128)}) custom-call(f32[8,32,1024]{2,1,0:T(8,128)S(1)} %get-tuple-element.6.acc_ref, f32[8,128]{1,0:T(8,128)S(1)} %get-tuple-element.7.halved_ref), custom_call_target="tpu_custom_call" | custom-call | tf_op jit(solution)/shard_map/output/pallas_call | solution.py:729
